TPU v7x, 128 devices: a whole 4x4x4 slice. The times are simulated.
128 devices in a mesh: sector: 16 (over y, x_lo, core), row: 8 (over z, x_hi).
Axes of the slice: x: 4 (x_hi: 2, x_lo: 2; x = x_hi * 2 + x_lo), y: 4, z: 4, core: 2. Of those that a mesh axis runs over, the one named last changes fastest.
Arguments:
- psi_sectors: bfloat16 [64, 16384, 256], P('sector', 'row'), may hold values from -1.25 to 1.25
- stiff_blocks: bfloat16 [128, 5, 128, 128], P('row'), as said below
- mass_blocks: bfloat16 [128, 5, 128, 128], P('row'), as said below
- harmonic_table: int32 [32], replicated, may hold values from 0 to 31, each once
Outputs:
- reduced_stiffness: float32 [32, 512, 512], P('sector', 'row')
- reduced_mass: float32 [32, 512, 512], P('sector', 'row')
Inputs may be any that keep to these rules, and one draw needn't show every extreme that they name: The stiffness is symmetric: stiff_blocks[i, 2 + d] is the transpose of stiff_blocks[i + d, 2 - d], and blocks whose column lies outside 0 to 127 are zero. `mass_blocks`: the mass is symmetric in the same way, and diagonally dominant with a positive diagonal, hence positive definite.
All inputs are finite; a program needn't handle non-finite values.
Results may differ from a plain program's by a relative error of at most 0.0049.
Values may be sent and summed in bfloat16 or wider, within the bound.
A program may use at most 128 MiB of HBM per device.

v0:
```python
import math

import jax
import jax.numpy as jnp
from jax import lax
from jax.sharding import PartitionSpec as P

B = 128
REACH = 2


def items_in_groups(x, axis, split_dim, concat_dim, work, item_dim, out_dim):
    items = jax.tree.leaves(x)[0].shape[item_dim]
    count = 2 if items % 2 == 0 else 1
    done = []
    for k in range(count):
        group = jax.tree.map(
            lambda a: lax.slice_in_dim(
                a, k * (items // count), (k + 1) * (items // count), axis=item_dim
            ),
            x,
        )
        done.append(
            work(
                lax.all_to_all(
                    group, axis, split_axis=split_dim, concat_axis=concat_dim, tiled=True
                )
            )
        )
    return jax.tree.map(lambda *parts: jnp.concatenate(parts, axis=out_dim), *done)


def padded(block, sides, width):
    for axis, dim in sides:
        count = lax.axis_size(axis)
        forward = [(i, i + 1) for i in range(count - 1)]
        backward = [(target, source) for source, target in forward]
        low = lax.ppermute(
            lax.slice_in_dim(block, block.shape[dim] - width, None, axis=dim), axis, forward
        )
        high = lax.ppermute(lax.slice_in_dim(block, 0, width, axis=dim), axis, backward)
        block = jnp.concatenate([low, block, high], axis=dim)
    return block


def split_up(x, dim, devices):
    before, after = (x.shape[:dim], x.shape[dim + 1 :])
    return jnp.moveaxis(x.reshape(*before, devices, -1, *after), dim, 0)


def summed_on_arrival(x, axis, dim):
    devices = lax.axis_size(axis)
    blocks = lax.all_to_all(split_up(x, dim, devices), axis, 0, 0, tiled=True)
    return jnp.sum(blocks.astype(jnp.float32), axis=0)


def in_one_piece(arrays, axis, dim, along):
    widths = [a.shape[along] for a in arrays]
    both = jnp.concatenate(arrays, axis=along)
    out = summed_on_arrival(both, axis, dim)
    return tuple(jnp.split(out, [sum(widths[:k]) for k in range(1, len(widths))], axis=along))


def coefficients(harmonic_table, sectors_all):
    sector_ids = jnp.arange(sectors_all, dtype=jnp.int32)
    half_count = sectors_all // 2
    second_freq = jnp.where(harmonic_table == 0, half_count, harmonic_table)
    first_phase = harmonic_table[:, None] * sector_ids[None, :] % sectors_all
    second_phase = second_freq[:, None] * sector_ids[None, :] % sectors_all
    angle_unit = 2.0 * math.pi / sectors_all
    first_angle = first_phase.astype(jnp.float32) * angle_unit
    second_angle = second_phase.astype(jnp.float32) * angle_unit
    zero_pair = (harmonic_table == 0)[:, None]
    low_scale = math.sqrt(1.0 / sectors_all)
    high_scale = math.sqrt(2.0 / sectors_all)
    first_row = jnp.where(zero_pair, low_scale, high_scale) * jnp.cos(first_angle)
    second = jnp.where(
        zero_pair, low_scale * jnp.cos(second_angle), high_scale * jnp.sin(second_angle)
    )
    return jnp.stack([first_row, second], axis=1).reshape(2 * harmonic_table.shape[0], sectors_all)


def per_device(psi_sectors, stiff_blocks, mass_blocks, harmonic_table):
    sec_dev, rows_dev, mode_count = psi_sectors.shape
    sectors_all = sec_dev * lax.axis_size("sector")
    dft_table = coefficients(harmonic_table, sectors_all)
    margin = REACH * B

    def transform(arrived):
        combined = jnp.einsum(
            "cs,srm->crm", dft_table, arrived.astype(jnp.float32), precision=lax.Precision.HIGHEST
        )
        return combined.astype(jnp.bfloat16)

    def columns_back(arrived):
        return lax.all_to_all(transform(arrived), "sector", split_axis=0, concat_axis=2, tiled=True)

    harmonics = items_in_groups(psi_sectors, "sector", 2, 0, columns_back, 1, 1)
    extended = padded(harmonics, (("row", 1),), margin)
    block_rows = rows_dev // B
    blocks_ext = extended.reshape(sec_dev, block_rows + 2 * REACH, B, mode_count)
    gathered = jnp.stack(
        [blocks_ext[:, offset : offset + block_rows] for offset in range(2 * REACH + 1)], axis=2
    )
    slot_dev = sec_dev // 2

    def paired(field_data):
        split = field_data.reshape(slot_dev, 2, rows_dev, mode_count)
        return split.transpose(0, 2, 1, 3).reshape(slot_dev, rows_dev, 2 * mode_count)

    def project_band(blocks):
        images = jnp.einsum(
            "ijab,cijbm->ciam", blocks, gathered, preferred_element_type=jnp.float32
        )
        return paired(images.astype(jnp.bfloat16).reshape(sec_dev, rows_dev, mode_count))

    left_basis = paired(harmonics)
    stiff_terms = jnp.einsum(
        "sra,srb->sab", left_basis, project_band(stiff_blocks), preferred_element_type=jnp.float32
    )
    mass_terms = jnp.einsum(
        "sra,srb->sab", left_basis, project_band(mass_blocks), preferred_element_type=jnp.float32
    )
    reduced_stiffness, reduced_mass = in_one_piece(
        (stiff_terms.astype(jnp.bfloat16), mass_terms.astype(jnp.bfloat16)), "row", 1, 0
    )
    return (reduced_stiffness, reduced_mass)


def solution(mesh):
    placed = (P("sector", "row", None), P("row", None, None, None), P("row", None, None, None), P())
    return jax.shard_map(
        per_device,
        mesh=mesh,
        in_specs=placed,
        out_specs=(P("sector", "row", None), P("sector", "row", None)),
        check_vma=False,
    )
```

profile of v0, /device:TPU:1, one launch (start us, length us, event | category | flops | bytes accessed | tf_op | source)
XLA Modules:
  0.0 286.9 jit_solution(13453881405923402012)
XLA Ops:
  0.6 4.6 %fusion.24 = (bf16[4,1024,256]{2,1,0:T(8,128)(2,1)}, bf16[4,1024,256]{2,1,0:T(8,128)(2,1)}) fusion(bf16[4,2048,256]{2,1,0:T(8,128)(2,1)} %param.4), kind=kLoop, calls=%fused_computation.51 | loop fusion | bytes 8388608 | tf_op jit(solution)/shard_map/slice | solution.py:18
  5.2 4.6 %copy.147 = bf16[4,1024,256]{1,0,2:T(4,128)(2,1)} copy(bf16[4,1024,256]{2,1,0:T(8,128)(2,1)} %get-tuple-element.7) | data formatting | bytes 4194304
  9.8 6.9 %all-to-all-start = ((bf16[4,1024,256]{1,0,2:T(4,128)(2,1)}), bf16[4,1024,256]{1,0,2:T(4,128)(2,1)}, u32[]{:S(2)}, u32[]{:S(2)}) async-start(bf16[4,1024,256]{1,0,2:T(4,128)(2,1)} %copy.147), calls=%async_computation | async-start | bytes 4194304 | tf_op jit(solution)/shard_map/all_to_all | solution.py:25
  16.7 4.5 %copy.148 = bf16[4,1024,256]{1,0,2:T(4,128)(2,1)} copy(bf16[4,1024,256]{2,1,0:T(8,128)(2,1)} %get-tuple-element.8) | data formatting | bytes 4194304
  21.3 22.5 %all-to-all-done = bf16[4,1024,256]{1,0,2:T(4,128)(2,1)} async-done(((bf16[4,1024,256]{1,0,2:T(4,128)(2,1)}), bf16[4,1024,256]{1,0,2:T(4,128)(2,1)}, u32[]{:S(2)}, u32[]{:S(2)}) %all-to-all-start) | async-done | bytes 2097184 | tf_op jit(solution)/shard_map/all_to_all | solution.py:25
  43.8 5.1 %all-to-all-start.2 = ((bf16[4,1024,256]{1,0,2:T(4,128)(2,1)}), bf16[4,1024,256]{1,0,2:T(4,128)(2,1)}, u32[]{:S(2)}, u32[]{:S(2)}) async-start(bf16[4,1024,256]{1,0,2:T(4,128)(2,1)} %copy.148), calls=%async_computation.2 | async-start | bytes 4194304 | tf_op jit(solution)/shard_map/all_to_all | solution.py:25
  49.2 2.2 copy.117
  51.4 3.0 %copy.118 = bf16[16,4,1024,16]{2,1,0,3:T(4,128)(2,1)} copy(bf16[16,4,1024,16]{2,3,0,1:T(8,128)(2,1)S(1)} %bitcast.103) | data formatting | bytes 4194304 | tf_op jit(solution)/shard_map/all_to_all | solution.py:25
  54.4 4.0 %all_to_all.58 = bf16[64,1024,16]{1,0,2:T(8,128)(2,1)} reshape(bf16[16,4,1024,16]{2,1,0,3:T(4,128)(2,1)} %copy.118) | data formatting | bytes 4194304 | tf_op jit(solution)/shard_map/all_to_all | solution.py:25
  58.4 3.4 %convolution_convert_fusion.1 = bf16[64,1024,16]{1,0,2:T(8,128)(2,1)S(1)} fusion(f32[64,64,1]{1,0,2:T(8,128)S(1)} %bitcast.110, bf16[64,1024,16]{1,0,2:T(8,128)(2,1)} %all_to_all.58), kind=kOutput, calls=%fused_computation.22 | convolution fusion | flops 806354944 | bytes 4210688 | tf_op jit(solution)/shard_map/cs,srm->crm/dot_general | solution.py:90
  61.8 2.5 copy.119
  64.3 11.8 %all-to-all-done.2 = bf16[4,1024,256]{1,0,2:T(4,128)(2,1)} async-done(((bf16[4,1024,256]{1,0,2:T(4,128)(2,1)}), bf16[4,1024,256]{1,0,2:T(4,128)(2,1)}, u32[]{:S(2)}, u32[]{:S(2)}) %all-to-all-start.2) | async-done | bytes 2097184 | tf_op jit(solution)/shard_map/all_to_all | solution.py:25
  76.1 5.1 %all-to-all-start.1 = ((bf16[64,1024,16]{1,2,0:T(8,128)(2,1)}), bf16[64,1024,16]{1,2,0:T(8,128)(2,1)}, u32[]{:S(2)}, u32[]{:S(2)}) async-start(bf16[64,1024,16]{1,2,0:T(8,128)(2,1)} %copy.119), calls=%async_computation.1 | async-start | bytes 4194304 | tf_op jit(solution)/shard_map/all_to_all | solution.py:96
  81.2 2.2 copy.122
  83.4 2.9 %copy.123 = bf16[16,4,1024,16]{2,1,0,3:T(4,128)(2,1)} copy(bf16[16,4,1024,16]{2,3,0,1:T(8,128)(2,1)S(1)} %bitcast.104) | data formatting | bytes 4194304 | tf_op jit(solution)/shard_map/all_to_all | solution.py:25
  86.3 4.0 %all_to_all.65 = bf16[64,1024,16]{1,0,2:T(8,128)(2,1)} reshape(bf16[16,4,1024,16]{2,1,0,3:T(4,128)(2,1)} %copy.123) | data formatting | bytes 4194304 | tf_op jit(solution)/shard_map/all_to_all | solution.py:25
  90.3 3.4 %convolution_convert_fusion = bf16[64,1024,16]{1,0,2:T(8,128)(2,1)S(1)} fusion(f32[64,64,1]{1,0,2:T(8,128)S(1)} %bitcast.111, bf16[64,1024,16]{1,0,2:T(8,128)(2,1)} %all_to_all.65), kind=kOutput, calls=%fused_computation.21 | convolution fusion | flops 806354944 | bytes 4210688 | tf_op jit(solution)/shard_map/cs,srm->crm/dot_general | solution.py:90
  93.7 2.5 copy.124
  96.2 12.2 %all-to-all-done.1 = bf16[64,1024,16]{1,2,0:T(8,128)(2,1)} async-done(((bf16[64,1024,16]{1,2,0:T(8,128)(2,1)}), bf16[64,1024,16]{1,2,0:T(8,128)(2,1)}, u32[]{:S(2)}, u32[]{:S(2)}) %all-to-all-start.1) | async-done | bytes 2097184 | tf_op jit(solution)/shard_map/all_to_all | solution.py:96
  108.3 5.1 %all-to-all-start.3 = ((bf16[64,1024,16]{1,2,0:T(8,128)(2,1)}), bf16[64,1024,16]{1,2,0:T(8,128)(2,1)}, u32[]{:S(2)}, u32[]{:S(2)}) async-start(bf16[64,1024,16]{1,2,0:T(8,128)(2,1)} %copy.124), calls=%async_computation.3 | async-start | bytes 4194304 | tf_op jit(solution)/shard_map/all_to_all | solution.py:96
  113.5 1.8 copy.120
  115.2 1.3 copy-done.2
  117.4 1.3 collective-permute-start.1
  118.7 21.9 %all-to-all-done.3 = bf16[64,1024,16]{1,2,0:T(8,128)(2,1)} async-done(((bf16[64,1024,16]{1,2,0:T(8,128)(2,1)}), bf16[64,1024,16]{1,2,0:T(8,128)(2,1)}, u32[]{:S(2)}, u32[]{:S(2)}) %all-to-all-start.3) | async-done | bytes 2097184 | tf_op jit(solution)/shard_map/all_to_all | solution.py:96
  140.6 2.0 copy.125
  142.7 4.4 %collective-permute-start = (bf16[4,256,256]{1,2,0:T(8,128)(2,1)S(1)}, bf16[4,256,256]{1,2,0:T(8,128)(2,1)S(1)}, u32[]{:S(2)}, u32[]{:S(2)}) collective-permute-start(bf16[4,256,256]{1,2,0:T(8,128)(2,1)S(1)} %slice.36), channel_id=1, source_target_pairs={{0,1},{1,2},{2,3},{3,4},{4,5},{5,6},{6,7},{8,9},{9,10},{10,11},{11... | collective-permute-start | bytes 1572872 | tf_op jit(solution)/shard_map/ppermute | solution.py:38
  147.2 2.5 pad_maximum_fusion.1
  149.6 2.5 collective-permute-done.1
  152.1 4.7 %collective-permute-done = bf16[4,256,256]{1,2,0:T(8,128)(2,1)S(1)} collective-permute-done((bf16[4,256,256]{1,2,0:T(8,128)(2,1)S(1)}, bf16[4,256,256]{1,2,0:T(8,128)(2,1)S(1)}, u32[]{:S(2)}, u32[]{:S(2)}) %collective-permute-start) | collective-permute-done | bytes 524320 | tf_op jit(solution)/shard_map/ppermute | solution.py:38
  156.8 2.9 pad_maximum_fusion
  159.7 8.0 %copy.128 = bf16[4,2560,256]{2,1,0:T(8,128)(2,1)} copy(bf16[4,2560,256]{1,2,0:T(8,128)(2,1)} %pad_maximum_fusion) | data formatting | bytes 10485760 | tf_op jit(solution)/shard_map/concatenate | solution.py:42
  167.7 13.9 %fusion.23 = (bf16[4,16,128,256]{3,2,1,0:T(8,128)(2,1)S(1)}, bf16[4,16,128,256]{3,2,1,0:T(8,128)(2,1)}, bf16[4,16,128,256]{3,2,1,0:T(8,128)(2,1)}, bf16[4,16,128,256]{3,2,1,0:T(8,128)(2,1)}, bf16[4,16,128,256]{3,2,1,0:T(8,128)(2,1)}) fusion(bf16[4,20,128,256]{3,2,1,0:T(8,128)(2,1)} %bitcast.93), kind=kLoop, calls=%fused_computation.50 | loop fusion | bytes 41943040 | tf_op jit(solution)/shard_map/slice | solution.py:103
  181.6 4.9 %fusion.6 = bf16[4,16,5,128,256]{4,3,2,0,1:T(8,128)(2,1)} fusion(bf16[4,16,128,256]{3,2,1,0:T(8,128)(2,1)} %get-tuple-element.6), kind=kLoop, calls=%fused_computation.15 | loop fusion | bytes 8388608
  186.5 2.4 fusion.5
  188.9 1.3 copy-done.5
  190.2 2.4 fusion.4
  192.6 1.3 copy-done.4
  193.9 2.3 fusion.3
  196.2 2.6 fusion.2
  198.8 10.7 %fusion = bf16[4,16,128,256]{3,2,0,1:T(8,128)(2,1)} fusion(bf16[4,16,5,128,256]{4,3,2,0,1:T(8,128)(2,1)} %fusion.2, bf16[16,5,128,128]{3,2,1,0:T(8,128)(2,1)S(1)} %copy-done), kind=kOutput, calls=%fused_computation.3 | convolution fusion | flops 2686451712 | bytes 27787264 | tf_op jit(solution)/shard_map/ijab,cijbm->ciam/dot_general | solution.py:112
  209.5 8.9 %fusion.1 = bf16[4,16,128,256]{3,2,0,1:T(8,128)(2,1)S(1)} fusion(bf16[4,16,5,128,256]{4,3,2,0,1:T(8,128)(2,1)} %fusion.2, bf16[16,5,128,128]{3,2,1,0:T(8,128)(2,1)S(1)} %copy-done.7), kind=kOutput, calls=%fused_computation.4 | convolution fusion | flops 2686451712 | bytes 27787264 | tf_op jit(solution)/shard_map/ijab,cijbm->ciam/dot_general | solution.py:112
  218.4 2.3 copy.137
  220.7 6.3 %copy.138 = bf16[2,2048,2,256]{1,3,2,0:T(8,128)(2,1)} copy(bf16[2,2048,2,256]{3,1,2,0:T(8,128)(2,1)} %bitcast.100) | data formatting | bytes 8388608 | tf_op jit(solution)/shard_map/transpose | solution.py:109
  227.0 4.7 %copy.134 = bf16[4,16,128,256]{3,2,1,0:T(8,128)(2,1)} copy(bf16[4,16,128,256]{3,2,0,1:T(8,128)(2,1)} %fusion) | data formatting | bytes 8388608 | tf_op jit(solution)/shard_map/convert_element_type | solution.py:115
  231.6 6.3 %copy.135 = bf16[2,2048,2,256]{1,3,2,0:T(8,128)(2,1)} copy(bf16[2,2048,2,256]{3,1,2,0:T(8,128)(2,1)} %bitcast.101) | data formatting | bytes 8388608 | tf_op jit(solution)/shard_map/transpose | solution.py:109
  238.0 6.0 %convolution_convert_fusion.2 = bf16[2,512,512]{2,1,0:T(8,128)(2,1)S(1)} fusion(bf16[2,2048,512]{1,2,0:T(8,128)(2,1)} %bitcast.106, bf16[2,2048,512]{1,2,0:T(8,128)(2,1)} %bitcast.108), kind=kOutput, calls=%fused_computation.23 | convolution fusion | flops 2148007936 | bytes 9437184 | tf_op jit(solution)/shard_map/sra,srb->sab/dot_general | solution.py:121
  243.9 2.4 convolution_convert_fusion.3
  246.7 39.1 %all_to_all.77 = bf16[8,4,64,512]{3,2,1,0:T(8,128)(2,1)S(1)} all-to-all(bf16[8,4,64,512]{3,2,1,0:T(8,128)(2,1)S(1)} %bitcast.105), channel_id=1, replica_groups=mesh['sector'=16,'row'=8] {'row'}, dimensions={0} | all-to-all | bytes 4194304 | tf_op jit(solution)/shard_map/all_to_all | solution.py:53
  (31 shorter events, 2.7 us)
Async XLA Ops:
  0.6 198.2 %copy-start = (bf16[16,5,128,128]{3,2,1,0:T(8,128)(2,1)S(1)}, bf16[16,5,128,128]{3,2,1,0:T(8,128)(2,1)}, u32[]{:S(2)}) copy-start(bf16[16,5,128,128]{3,2,1,0:T(8,128)(2,1)} %param.5) | copy-start | bytes 7864324
  9.8 34.0 %all-to-all-start = ((bf16[4,1024,256]{1,0,2:T(4,128)(2,1)}), bf16[4,1024,256]{1,0,2:T(4,128)(2,1)}, u32[]{:S(2)}, u32[]{:S(2)}) async-start(bf16[4,1024,256]{1,0,2:T(4,128)(2,1)} %copy.147), calls=%async_computation | async-start | bytes 4194304 | tf_op jit(solution)/shard_map/all_to_all | solution.py:25
  16.7 32.2 %copy-start.10 = (s32[32]{0:T(128)S(1)}, s32[32]{0:T(128)}, u32[]{:S(2)}) copy-start(s32[32]{0:T(128)} %param.7) | copy-start | bytes 388
  43.8 32.3 %all-to-all-start.2 = ((bf16[4,1024,256]{1,0,2:T(4,128)(2,1)}), bf16[4,1024,256]{1,0,2:T(4,128)(2,1)}, u32[]{:S(2)}, u32[]{:S(2)}) async-start(bf16[4,1024,256]{1,0,2:T(4,128)(2,1)} %copy.148), calls=%async_computation.2 | async-start | bytes 4194304 | tf_op jit(solution)/shard_map/all_to_all | solution.py:25
  76.1 32.3 %all-to-all-start.1 = ((bf16[64,1024,16]{1,2,0:T(8,128)(2,1)}), bf16[64,1024,16]{1,2,0:T(8,128)(2,1)}, u32[]{:S(2)}, u32[]{:S(2)}) async-start(bf16[64,1024,16]{1,2,0:T(8,128)(2,1)} %copy.119), calls=%async_computation.1 | async-start | bytes 4194304 | tf_op jit(solution)/shard_map/all_to_all | solution.py:96
  108.3 32.3 %all-to-all-start.3 = ((bf16[64,1024,16]{1,2,0:T(8,128)(2,1)}), bf16[64,1024,16]{1,2,0:T(8,128)(2,1)}, u32[]{:S(2)}, u32[]{:S(2)}) async-start(bf16[64,1024,16]{1,2,0:T(8,128)(2,1)} %copy.124), calls=%async_computation.3 | async-start | bytes 4194304 | tf_op jit(solution)/shard_map/all_to_all | solution.py:96
  115.2 1.3 copy-start.2
  117.4 34.7 %collective-permute-start.1 = (bf16[4,256,256]{1,2,0:T(8,128)(2,1)}, bf16[4,256,256]{1,2,0:T(8,128)(2,1)S(1)}, u32[]{:S(2)}, u32[]{:S(2)}) collective-permute-start(bf16[4,256,256]{1,2,0:T(8,128)(2,1)} %slice.37), channel_id=1, source_target_pairs={{1,0},{2,1},{3,2},{4,3},{5,4},{6,5},{7,6},{9,8},{10,9},{11,10},{12... | collective-permute-start | bytes 1572872 | tf_op jit(solution)/shard_map/ppermute | solution.py:41
  140.6 6.5 %copy-start.3 = (bf16[4,1024,16,16]{1,3,2,0:T(8,128)(2,1)S(1)}, bf16[4,1024,16,16]{1,3,2,0:T(8,128)(2,1)}, u32[]{:S(2)}) copy-start(bf16[4,1024,16,16]{1,3,2,0:T(8,128)(2,1)} %copy-done.2) | copy-start | bytes 6291460
  142.7 14.1 %collective-permute-start = (bf16[4,256,256]{1,2,0:T(8,128)(2,1)S(1)}, bf16[4,256,256]{1,2,0:T(8,128)(2,1)S(1)}, u32[]{:S(2)}, u32[]{:S(2)}) collective-permute-start(bf16[4,256,256]{1,2,0:T(8,128)(2,1)S(1)} %slice.36), channel_id=1, source_target_pairs={{0,1},{1,2},{2,3},{3,4},{4,5},{5,6},{6,7},{8,9},{9,10},{10,11},{11... | collective-permute-start | bytes 1572872 | tf_op jit(solution)/shard_map/ppermute | solution.py:38
  181.6 4.9 %copy-start.6 = (bf16[4,16,128,256]{3,2,1,0:T(8,128)(2,1)S(1)}, bf16[4,16,128,256]{3,2,1,0:T(8,128)(2,1)}, u32[]{:S(2)}) copy-start(bf16[4,16,128,256]{3,2,1,0:T(8,128)(2,1)} %get-tuple-element.5) | copy-start | bytes 12582916
  186.5 3.7 %copy-start.5 = (bf16[4,16,128,256]{3,2,1,0:T(8,128)(2,1)S(1)}, bf16[4,16,128,256]{3,2,1,0:T(8,128)(2,1)}, u32[]{:S(2)}) copy-start(bf16[4,16,128,256]{3,2,1,0:T(8,128)(2,1)} %get-tuple-element.4) | copy-start | bytes 12582916
  190.2 3.7 %copy-start.4 = (bf16[4,16,128,256]{3,2,1,0:T(8,128)(2,1)S(1)}, bf16[4,16,128,256]{3,2,1,0:T(8,128)(2,1)}, u32[]{:S(2)}) copy-start(bf16[4,16,128,256]{3,2,1,0:T(8,128)(2,1)} %get-tuple-element.3) | copy-start | bytes 12582916
  198.8 10.7 %copy-start.7 = (bf16[16,5,128,128]{3,2,1,0:T(8,128)(2,1)S(1)}, bf16[16,5,128,128]{3,2,1,0:T(8,128)(2,1)}, u32[]{:S(2)}) copy-start(bf16[16,5,128,128]{3,2,1,0:T(8,128)(2,1)} %param.6) | copy-start | bytes 7864324
  237.9 6.0 %copy-start.8 = (bf16[2,2,2048,256]{2,3,1,0:T(8,128)(2,1)S(1)}, bf16[2,2,2048,256]{2,3,1,0:T(8,128)(2,1)}, u32[]{:S(2)}) copy-start(bf16[2,2,2048,256]{2,3,1,0:T(8,128)(2,1)} %pad_maximum_fusion.1) | copy-start | bytes 12582916
  238.0 6.0 %copy-start.9 = (bf16[2,2048,2,256]{1,3,2,0:T(8,128)(2,1)S(1)}, bf16[2,2048,2,256]{1,3,2,0:T(8,128)(2,1)}, u32[]{:S(2)}) copy-start(bf16[2,2048,2,256]{1,3,2,0:T(8,128)(2,1)} %copy.135) | copy-start | bytes 12582916
  246.5 40.4 %copy-start.1 = (bf16[16,5,128,128]{3,2,1,0:T(8,128)(2,1)S(1)}, bf16[16,5,128,128]{3,2,1,0:T(8,128)(2,1)}, u32[]{:S(2)}) copy-start(bf16[16,5,128,128]{3,2,1,0:T(8,128)(2,1)} %param.5) | copy-start | bytes 7864324
where the time goes:
time: 289 us; the launch traced here: 287 us
  local copies, waits for them, and re-layouts  103 us (36%)
  waiting for transfers between devices  75.6 us (26%)
  blocking collectives  39.1 us (14%)
  matrix products  34.7 us (12%)
  starting transfers between devices  28 us (10%)
  other arithmetic  6.03 us (2%)
    all_to_all x1, blocking collectives, summed_on_arrival(): blocks = lax.all_to_all(split_up(x, dim, devices), axis, 0, 0, tiled=True)  39.1 us
    all_to_all x2, waiting for transfers between devices, items_in_groups(): lax.all_to_all(group, axis, split_axis=split_dim, concat_axis=concat_dim,...  34.3 us
    all_to_all x2, waiting for transfers between devices, columns_back(): lax.all_to_all(transform(arrived), 'sector', split_axis=0, concat_axis=2,...  34.1 us
    unnamed x28, local copies, waits for them, and re-layouts  25.1 us
    dot_general x2, matrix products, project_band(): jnp.einsum('ijab,cijbm->ciam', blocks, gathered, preferred_element_type=j...  19.6 us
    all_to_all x6, local copies, waits for them, and re-layouts, items_in_groups(): lax.all_to_all(group, axis, split_axis=split_dim, concat_axis=concat_dim,...  18.3 us
    slice x1, local copies, waits for them, and re-layouts, per_device(): blocks_ext[:, offset:offset + block_rows]  13.9 us
    transpose x2, local copies, waits for them, and re-layouts, paired(): split.transpose(0, 2, 1, 3).reshape(slot_dev, rows_dev, 2 * mode_count)  12.6 us
  transfers between devices with their start and end apart: 6, of which 6 were waited for; matrix products, arithmetic and copies ran while one was open for 12% of the time, Pallas kernels for 0%

commit v1 on v0

v1 whole, which is shorter than its diff:
```python
import functools
import math

import jax
import jax.numpy as jnp
from jax import lax
from jax.experimental import pallas as pl
from jax.experimental.pallas import tpu as pltpu
from jax.sharding import PartitionSpec as P

MESH = pl.DeviceIdType.MESH
B = 128
M = 256
NBAND = 5
ROWS_DEV = 2048
SEG = 1024
CHUNK = 256
NCHUNK = 4
PIECE = 32
TILE = 16
SLOTS_DEV = 4
ORDER = (3, 0, 1, 2)
HALO = 256
SECTOR_OFFSETS = tuple(
    (dy, dx, dc) for dy in (2, 1, 3, 0) for dx in (1, 0) for dc in (0, 1) if dy or dx or dc
)
OWNER_OFFSETS = tuple((dy, dc) for dy in (2, 1, 3, 0) for dc in (0, 1) if dy or dc)


def coefficients(harmonic_table, sectors_all):
    sector_ids = jnp.arange(sectors_all, dtype=jnp.int32)
    half_count = sectors_all // 2
    second_freq = jnp.where(harmonic_table == 0, half_count, harmonic_table)
    first_phase = harmonic_table[:, None] * sector_ids[None, :] % sectors_all
    second_phase = second_freq[:, None] * sector_ids[None, :] % sectors_all
    angle_unit = 2.0 * math.pi / sectors_all
    first_angle = first_phase.astype(jnp.float32) * angle_unit
    second_angle = second_phase.astype(jnp.float32) * angle_unit
    zero_pair = (harmonic_table == 0)[:, None]
    low_scale = math.sqrt(1.0 / sectors_all)
    high_scale = math.sqrt(2.0 / sectors_all)
    first_row = jnp.where(zero_pair, low_scale, high_scale) * jnp.cos(first_angle)
    second = jnp.where(
        zero_pair, low_scale * jnp.cos(second_angle), high_scale * jnp.sin(second_angle)
    )
    return jnp.concatenate([first_row, second], axis=0)


def kernel(
    psi, stiff, mass, table, out_k, out_m,
    arrived, sent, fields, lift, bands, images, total, parts, pieces,
    load_sem, s1, r1, s2, r2, sh, rh, s3, r3,
):
    sec = lax.axis_index("sector")
    row = lax.axis_index("row")
    y, xl, core = sec // 4, (sec // 2) % 2, sec % 2
    turn = y * 2 + core
    seg = row * 2 + xl

    def device(y_, xl_, core_, row_):
        return {"sector": y_ * 4 + xl_ * 2 + core_, "row": row_}

    loads = []
    for m, src in enumerate((stiff, mass)):
        for k in range(NBAND):
            copy = pltpu.make_async_copy(
                src.at[pl.ds(pl.multiple_of(xl * 8, 8), 8), k],
                bands.at[:, pl.ds(m * B, B), pl.ds(k * B, B)],
                load_sem.at[m, k],
            )
            copy.start()
            loads.append(copy)

    barrier = pltpu.get_barrier_semaphore()
    count = 0
    for dy, dx, dc in SECTOR_OFFSETS:
        pl.semaphore_signal(
            barrier, inc=1, device_id_type=MESH,
            device_id=device((y + dy) % 4, (xl + dx) % 2, (core + dc) % 2, row),
        )
        count += 1
    for dr in range(1, 8):
        for dx in range(2):
            pl.semaphore_signal(
                barrier, inc=1, device_id_type=MESH,
                device_id=device(y, (xl + dx) % 2, core, (row + dr) % 8),
            )
            count += 1
    pl.semaphore_wait(barrier, count)

    def rows_of(xl_, turn_, q):
        return pl.ds(pl.multiple_of(xl_ * SEG + q * CHUNK + turn_ * PIECE, PIECE), PIECE)

    for q in ORDER:
        for dy, dx, dc in SECTOR_OFFSETS:
            y_, xl_, core_ = (y + dy) % 4, (xl + dx) % 2, (core + dc) % 2
            pltpu.make_async_remote_copy(
                src_ref=psi.at[:, rows_of(xl_, y_ * 2 + core_, q), :],
                dst_ref=arrived.at[q, pl.ds(sec * 4, 4)],
                send_sem=s1.at[q],
                recv_sem=r1.at[q],
                device_id=device(y_, xl_, core_, row),
                device_id_type=MESH,
            ).start()
        pltpu.make_async_copy(
            psi.at[:, rows_of(xl, turn, q), :], arrived.at[q, pl.ds(sec * 4, 4)], r1.at[q]
        ).start()

    coef = table[...]
    coef_hi = coef.astype(jnp.bfloat16)
    coef_lo = (coef - coef_hi.astype(jnp.float32)).astype(jnp.bfloat16)
    quarter = 256

    def spread(n, _):
        i = lax.broadcasted_iota(jnp.int32, (quarter, 64), 0) + n * quarter
        g = i // TILE
        e, t, k = g % 2, (g // 2) % 8, g // 16
        slot = (t // 2) * 8 + (k // 2) * 4 + (t % 2) * 2 + k % 2
        want = e * 32 + slot
        pick = (lax.broadcasted_iota(jnp.int32, (quarter, 64), 1) == want).astype(jnp.bfloat16)
        col = lax.broadcasted_iota(jnp.int32, (64, 1024), 1) // TILE
        wide = (lax.broadcasted_iota(jnp.int32, (64, 1024), 0) == col).astype(jnp.bfloat16)
        same = (
            lax.broadcasted_iota(jnp.int32, (quarter, 1024), 0) % TILE
            == lax.broadcasted_iota(jnp.int32, (quarter, 1024), 1) % TILE
        )
        for h, part in enumerate((coef_hi, coef_lo)):
            chosen = jnp.dot(pick, part, preferred_element_type=jnp.float32).astype(jnp.bfloat16)
            full = jnp.dot(chosen, wide, preferred_element_type=jnp.float32)
            lift[h, pl.ds(pl.multiple_of(n * quarter, quarter), quarter), :] = jnp.where(
                same, full, 0.0
            ).astype(jnp.bfloat16)
        return 0

    lax.fori_loop(0, 4, spread, 0)

    def send_fields(k, q):
        mine = pl.ds(pl.multiple_of(HALO + q * CHUNK + turn * PIECE, PIECE), PIECE)
        for dy, dc in OWNER_OFFSETS:
            y_, core_ = (y + dy) % 4, (core + dc) % 2
            pltpu.make_async_remote_copy(
                src_ref=sent.at[q, pl.ds(k * 16 + (y_ * 2 + core_) * 2, 2)],
                dst_ref=fields.at[k, :, mine, :],
                send_sem=s2.at[k],
                recv_sem=r2.at[k, q],
                device_id=device(y_, xl, core_, row),
                device_id_type=MESH,
            ).start()
        pltpu.make_async_copy(
            sent.at[q, pl.ds(k * 16 + turn * 2, 2)], fields.at[k, :, mine, :], r2.at[k, q]
        ).start()

    for q in ORDER:
        pltpu.make_async_copy(arrived.at[q], arrived.at[q], r1.at[q]).wait()

        def transform(h, _):
            rows = pl.ds(pl.multiple_of(h * TILE, TILE), TILE)
            x = arrived[q, :, rows, :].reshape(64 * TILE, M)
            for n in range(2):
                at = pl.ds(n * 512, 512)
                out = jnp.dot(lift[0, at, :], x, preferred_element_type=jnp.float32)
                out += jnp.dot(lift[1, at, :], x, preferred_element_type=jnp.float32)
                sent[q, pl.ds(n * 32, 32), rows, :] = out.astype(jnp.bfloat16).reshape(
                    32, TILE, M
                )
            return 0

        lax.fori_loop(0, PIECE // TILE, transform, 0)
        send_fields(0, q)

    for copy in loads:
        copy.wait()

    def process(k, q, first):
        for b in range(2):
            i = 2 * q + b
            for e in range(2):
                window = fields[k, e, pl.ds(i * B, NBAND * B), :]
                w = jnp.dot(bands[i], window, preferred_element_type=jnp.float32)
                w = w.astype(jnp.bfloat16)
                images[pl.ds(b * B, B), pl.ds(e * M, M)] = w[:B]
                images[pl.ds(b * B, B), pl.ds(2 * M + e * M, M)] = w[B:]
        for e in range(2):
            left = fields[k, e, pl.ds(HALO + q * CHUNK, CHUNK), :]
            part = lax.dot_general(
                left, images[...], (((0,), (0,)), ((), ())), preferred_element_type=jnp.float32
            )
            at = pl.ds(e * M, M)
            if first:
                total[at, :] = part
            else:
                total[at, :] += part

    def arrival(k, q):
        whole = fields.at[k, :, pl.ds(0, CHUNK), :]
        pltpu.make_async_copy(whole, whole, r2.at[k, q]).wait()

    def halo(k, up):
        to = (seg + (1 if up else 15)) % 16
        src, dst = (SEG, 0) if up else (HALO, HALO + SEG)
        side = 0 if up else 1
        return pltpu.make_async_remote_copy(
            src_ref=fields.at[k, :, pl.ds(src, HALO), :],
            dst_ref=fields.at[k, :, pl.ds(dst, HALO), :],
            send_sem=sh.at[k, side],
            recv_sem=rh.at[k, side],
            device_id=device(y, to % 2, core, to // 2),
            device_id_type=MESH,
        )

    def slot(k):
        if k + 1 < SLOTS_DEV:
            for q in ORDER:
                send_fields(k + 1, q)
        arrival(k, 3)
        halo(k, True).start()
        arrival(k, 0)
        halo(k, False).start()
        arrival(k, 1)
        halo(k, True).wait_recv()
        process(k, 0, True)
        arrival(k, 2)
        process(k, 1, False)
        process(k, 2, False)
        halo(k, False).wait_recv()
        process(k, 3, False)
        parts[k] = total[...].astype(jnp.bfloat16)
        owner = k // 2
        for dr in (4, 5, 3, 6, 2, 7, 1):
            row_ = (row + dr) % 8
            pltpu.make_async_remote_copy(
                src_ref=parts.at[k, pl.ds(pl.multiple_of(row_ * 64, 64), 64), :],
                dst_ref=pieces.at[k % 2, seg],
                send_sem=s3.at[k, 0],
                recv_sem=r3.at[k % 2],
                device_id=device(y, owner, core, row_),
                device_id_type=MESH,
            ).start()
        own = parts.at[k, pl.ds(pl.multiple_of(row * 64, 64), 64), :]

        @pl.when(xl == owner)
        def _():
            pltpu.make_async_copy(own, pieces.at[k % 2, seg], r3.at[k % 2]).start()

        @pl.when(xl != owner)
        def _():
            pltpu.make_async_remote_copy(
                src_ref=own,
                dst_ref=pieces.at[k % 2, seg],
                send_sem=s3.at[k, 1],
                recv_sem=r3.at[k % 2],
                device_id=device(y, 1 - xl, core, row),
                device_id_type=MESH,
            ).start()

    for k in range(SLOTS_DEV):
        slot(k)

    for k in range(2):
        pltpu.make_async_copy(pieces.at[k], pieces.at[k], r3.at[k]).wait()
        acc = pieces[k, 0].astype(jnp.float32)
        for n in range(1, 16):
            acc += pieces[k, n].astype(jnp.float32)
        out_k[k] = acc[:, :512]
        out_m[k] = acc[:, 512:]

    for q in range(NCHUNK):
        gone = arrived.at[q, pl.ds(0, 60)]
        pltpu.make_async_copy(gone, gone, s1.at[q]).wait()
    for k in range(SLOTS_DEV):
        gone = sent.at[pl.ds(0, 4), pl.ds(0, 14)]
        pltpu.make_async_copy(gone, gone, s2.at[k]).wait()
        halo(k, True).wait_send()
        halo(k, False).wait_send()
        gone = parts.at[k, pl.ds(0, 448), :]
        pltpu.make_async_copy(gone, gone, s3.at[k, 0]).wait()

        @pl.when(xl != k // 2)
        def _():
            gone = parts.at[k, pl.ds(0, 64), :]
            pltpu.make_async_copy(gone, gone, s3.at[k, 1]).wait()


def per_device(psi_sectors, stiff_blocks, mass_blocks, harmonic_table):
    table = coefficients(harmonic_table, 64)
    anywhere = pl.BlockSpec(memory_space=pl.ANY)
    vmem = pl.BlockSpec(memory_space=pltpu.VMEM)
    bf16, f32 = jnp.bfloat16, jnp.float32
    dma = pltpu.SemaphoreType.DMA
    return pl.pallas_call(
        kernel,
        out_shape=(
            jax.ShapeDtypeStruct((2, 64, 512), f32),
            jax.ShapeDtypeStruct((2, 64, 512), f32),
        ),
        in_specs=[anywhere, anywhere, anywhere, vmem],
        out_specs=(vmem, vmem),
        scratch_shapes=[
            pltpu.VMEM((NCHUNK, 64, PIECE, M), bf16),
            pltpu.VMEM((NCHUNK, 64, PIECE, M), bf16),
            pltpu.VMEM((SLOTS_DEV, 2, SEG + 2 * HALO, M), bf16),
            pltpu.VMEM((2, 1024, 1024), bf16),
            pltpu.VMEM((8, 2 * B, NBAND * B), bf16),
            pltpu.VMEM((CHUNK, 4 * M), bf16),
            pltpu.VMEM((2 * M, 4 * M), f32),
            pltpu.VMEM((SLOTS_DEV, 2 * M, 4 * M), bf16),
            pltpu.VMEM((2, 16, 64, 4 * M), bf16),
            dma((2, NBAND)),
            dma((NCHUNK,)),
            dma((NCHUNK,)),
            dma((SLOTS_DEV,)),
            dma((SLOTS_DEV, NCHUNK)),
            dma((SLOTS_DEV, 2)),
            dma((SLOTS_DEV, 2)),
            dma((SLOTS_DEV, 2)),
            dma((2,)),
        ],
        compiler_params=pltpu.CompilerParams(
            collective_id=0, has_side_effects=True, vmem_limit_bytes=60 * 1024 * 1024
        ),
        name="reduce_sectors",
    )(psi_sectors, stiff_blocks, mass_blocks, table)


def solution(mesh):
    placed = (P("sector", "row", None), P("row", None, None, None), P("row", None, None, None), P())
    return jax.shard_map(
        per_device,
        mesh=mesh,
        in_specs=placed,
        out_specs=(P("sector", "row", None), P("sector", "row", None)),
        check_vma=False,
    )
```

time: 289 us -> 205 us (0.71)
  the two profiles are of different devices: /device:TPU:1 before, /device:TPU:26 now
where the time goes in v1:
time: 205 us
  Pallas kernels  197 us (96%)
  other arithmetic  3.46 us (2%)
  local copies, waits for them, and re-layouts  3.34 us (2%)
    pallas_call x1, Pallas kernels, per_device(): pl.pallas_call(kernel, out_shape=(jax.ShapeDtypeStruct((2, 64, 512), f32)...  197 us

profile of v1, /device:TPU:26, one launch (start us, length us, event | category | flops | bytes accessed | tf_op | source)
XLA Modules:
  0.0 204.7 jit_solution(15612377332389579165)
XLA Ops:
  0.6 0.7 broadcast_select_fusion.1
  1.3 0.7 broadcast_compare_fusion
  1.9 0.7 broadcast_select_fusion
  2.6 0.9 fusion.4
  3.5 0.6 pad_maximum_fusion.table
  4.1 197.3 %reduce_sectors.1 = (f32[2,64,512]{2,1,0:T(8,128)}, f32[2,64,512]{2,1,0:T(8,128)}) custom-call(bf16[4,2048,256]{2,1,0:T(8,128)(2,1)} %psi.1, bf16[16,5,128,128]{3,2,1,0:T(8,128)(2,1)} %stiff.1, bf16[16,5,128,128]{3,2,1,0:T(8,128)(2,1)} %mass.1, f32[64,64]{1,0:T(8,128)} %pad_maximum_fusion.table), custom_call_target="tpu_custom_call" | custom-call | tf_op jit(solution)/shard_map/reduce_sectors/pallas_call | solution.py:290
  201.4 1.7 copy.8
  203.0 1.7 copy.9

commit v2 on v1

--- a/solution.py
+++ b/solution.py
@@ -21,41 +21,41 @@
 SLOTS_DEV = 4
 ORDER = (3, 0, 1, 2)
 HALO = 256
+SECTORS = 64
+SLOTS = 32
 SECTOR_OFFSETS = tuple(
     (dy, dx, dc) for dy in (2, 1, 3, 0) for dx in (1, 0) for dc in (0, 1) if dy or dx or dc
 )
 OWNER_OFFSETS = tuple((dy, dc) for dy in (2, 1, 3, 0) for dc in (0, 1) if dy or dc)
 
 
-def coefficients(harmonic_table, sectors_all):
-    sector_ids = jnp.arange(sectors_all, dtype=jnp.int32)
-    half_count = sectors_all // 2
-    second_freq = jnp.where(harmonic_table == 0, half_count, harmonic_table)
-    first_phase = harmonic_table[:, None] * sector_ids[None, :] % sectors_all
-    second_phase = second_freq[:, None] * sector_ids[None, :] % sectors_all
-    angle_unit = 2.0 * math.pi / sectors_all
-    first_angle = first_phase.astype(jnp.float32) * angle_unit
-    second_angle = second_phase.astype(jnp.float32) * angle_unit
-    zero_pair = (harmonic_table == 0)[:, None]
-    low_scale = math.sqrt(1.0 / sectors_all)
-    high_scale = math.sqrt(2.0 / sectors_all)
-    first_row = jnp.where(zero_pair, low_scale, high_scale) * jnp.cos(first_angle)
-    second = jnp.where(
-        zero_pair, low_scale * jnp.cos(second_angle), high_scale * jnp.sin(second_angle)
-    )
-    return jnp.concatenate([first_row, second], axis=0)
+def coefficients(table):
+    shape = (2 * SLOTS, SECTORS)
+    line = lax.broadcasted_iota(jnp.int32, shape, 0)
+    sector = lax.broadcasted_iota(jnp.int32, shape, 1)
+    pair = jnp.zeros(shape, jnp.int32)
+    for j in range(SLOTS):
+        pair = jnp.where(line % SLOTS == j, table[j], pair)
+    first = line < SLOTS
+    zero = pair == 0
+    freq = jnp.where(jnp.logical_and(zero, jnp.logical_not(first)), SECTORS // 2, pair)
+    shift = jnp.where(jnp.logical_or(first, zero), 0, 3 * SECTORS // 4)
+    phase = (freq * sector + shift) % SECTORS
+    wave = jnp.cos(phase.astype(jnp.float32) * (2.0 * math.pi / SECTORS))
+    return jnp.where(zero, math.sqrt(1.0 / SECTORS), math.sqrt(2.0 / SECTORS)) * wave
 
 
 def kernel(
     psi, stiff, mass, table, out_k, out_m,
-    arrived, sent, fields, lift, bands, images, total, parts, pieces,
-    load_sem, s1, r1, s2, r2, sh, rh, s3, r3,
+    arrived, sent, fields, lift, bands, images, total, parts, stage, middle, pieces, last,
+    load_sem, s1, r1, s2, r2, sh, rh, s3, r3, s4, r4, s5, r5,
 ):
     sec = lax.axis_index("sector")
     row = lax.axis_index("row")
     y, xl, core = sec // 4, (sec // 2) % 2, sec % 2
     turn = y * 2 + core
     seg = row * 2 + xl
+    z, xh = row // 2, row % 2
 
     def device(y_, xl_, core_, row_):
         return {"sector": y_ * 4 + xl_ * 2 + core_, "row": row_}
@@ -86,7 +86,8 @@
                 device_id=device(y, (xl + dx) % 2, core, (row + dr) % 8),
             )
             count += 1
-    pl.semaphore_wait(barrier, count)
+    with jax.named_scope("barrier"):
+        pl.semaphore_wait(barrier, count)
 
     def rows_of(xl_, turn_, q):
         return pl.ds(pl.multiple_of(xl_ * SEG + q * CHUNK + turn_ * PIECE, PIECE), PIECE)
@@ -106,7 +107,7 @@
             psi.at[:, rows_of(xl, turn, q), :], arrived.at[q, pl.ds(sec * 4, 4)], r1.at[q]
         ).start()
 
-    coef = table[...]
+    coef = coefficients(table)
     coef_hi = coef.astype(jnp.bfloat16)
     coef_lo = (coef - coef_hi.astype(jnp.float32)).astype(jnp.bfloat16)
     quarter = 256
@@ -115,7 +116,7 @@
         i = lax.broadcasted_iota(jnp.int32, (quarter, 64), 0) + n * quarter
         g = i // TILE
         e, t, k = g % 2, (g // 2) % 8, g // 16
-        slot = (t // 2) * 8 + (k // 2) * 4 + (t % 2) * 2 + k % 2
+        slot = (t // 2) * 8 + ((k // 2 + t) % 2) * 4 + (t % 2) * 2 + k % 2
         want = e * 32 + slot
         pick = (lax.broadcasted_iota(jnp.int32, (quarter, 64), 1) == want).astype(jnp.bfloat16)
         col = lax.broadcasted_iota(jnp.int32, (64, 1024), 1) // TILE
@@ -132,7 +133,8 @@
             ).astype(jnp.bfloat16)
         return 0
 
-    lax.fori_loop(0, 4, spread, 0)
+    with jax.named_scope("spread"):
+        lax.fori_loop(0, 4, spread, 0)
 
     def send_fields(k, q):
         mine = pl.ds(pl.multiple_of(HALO + q * CHUNK + turn * PIECE, PIECE), PIECE)
@@ -151,7 +153,8 @@
         ).start()
 
     for q in ORDER:
-        pltpu.make_async_copy(arrived.at[q], arrived.at[q], r1.at[q]).wait()
+        with jax.named_scope(f"wait_one#q={q}"):
+            pltpu.make_async_copy(arrived.at[q], arrived.at[q], r1.at[q]).wait()
 
         def transform(h, _):
             rows = pl.ds(pl.multiple_of(h * TILE, TILE), TILE)
@@ -165,7 +168,8 @@
                 )
             return 0
 
-        lax.fori_loop(0, PIECE // TILE, transform, 0)
+        with jax.named_scope(f"transform#q={q}"):
+            lax.fori_loop(0, PIECE // TILE, transform, 0)
         send_fields(0, q)
 
     for copy in loads:
@@ -193,7 +197,8 @@
 
     def arrival(k, q):
         whole = fields.at[k, :, pl.ds(0, CHUNK), :]
-        pltpu.make_async_copy(whole, whole, r2.at[k, q]).wait()
+        with jax.named_scope(f"wait_two#k={k}#q={q}"):
+            pltpu.make_async_copy(whole, whole, r2.at[k, q]).wait()
 
     def halo(k, up):
         to = (seg + (1 if up else 15)) % 16
@@ -209,60 +214,134 @@
         )
 
     def slot(k):
-        if k + 1 < SLOTS_DEV:
+        if k + 2 < SLOTS_DEV:
             for q in ORDER:
-                send_fields(k + 1, q)
+                send_fields(k + 2, q)
         arrival(k, 3)
         halo(k, True).start()
         arrival(k, 0)
         halo(k, False).start()
         arrival(k, 1)
-        halo(k, True).wait_recv()
-        process(k, 0, True)
+        with jax.named_scope(f"wait_low#k={k}"):
+            halo(k, True).wait_recv()
+        with jax.named_scope(f"process#k={k}#q=0"):
+            process(k, 0, True)
         arrival(k, 2)
-        process(k, 1, False)
-        process(k, 2, False)
-        halo(k, False).wait_recv()
-        process(k, 3, False)
-        parts[k] = total[...].astype(jnp.bfloat16)
-        owner = k // 2
-        for dr in (4, 5, 3, 6, 2, 7, 1):
-            row_ = (row + dr) % 8
-            pltpu.make_async_remote_copy(
-                src_ref=parts.at[k, pl.ds(pl.multiple_of(row_ * 64, 64), 64), :],
-                dst_ref=pieces.at[k % 2, seg],
-                send_sem=s3.at[k, 0],
-                recv_sem=r3.at[k % 2],
-                device_id=device(y, owner, core, row_),
-                device_id_type=MESH,
+        with jax.named_scope(f"process#k={k}#q=1"):
+            process(k, 1, False)
+        with jax.named_scope(f"process#k={k}#q=2"):
+            process(k, 2, False)
+        with jax.named_scope(f"wait_high#k={k}"):
+            halo(k, False).wait_recv()
+        with jax.named_scope(f"process#k={k}#q=3"):
+            process(k, 3, False)
+        with jax.named_scope(f"narrow#k={k}"):
+            parts[k] = total[...].astype(jnp.bfloat16)
+        if k < SLOTS_DEV - 1:
+            for dz in (2, 1, 3):
+                column(k, dz).start()
+        else:
+            for dr in (4, 5, 3, 6, 2, 7, 1):
+                direct(dr).start()
+
+            @pl.when(xl == owner(k))
+            def _():
+                pltpu.make_async_copy(direct_part(row), last.at[seg], r4).start()
+
+            @pl.when(xl != owner(k))
+            def _():
+                direct(0).start()
+
+    def owner(k):
+        return (k // 2 + core) % 2
+
+    def column(k, dz):
+        z_ = (z + dz) % 4
+        return pltpu.make_async_remote_copy(
+            src_ref=parts.at[k, pl.ds(pl.multiple_of(z_ * 128, 128), 128), :],
+            dst_ref=stage.at[k, (3 - dz)],
+            send_sem=s3.at[k],
+            recv_sem=r3.at[k],
+            device_id=device(y, xl, core, z_ * 2 + xh),
+            device_id_type=MESH,
+        )
+
+    def across(k, dh):
+        xh_ = (xh + dh) % 2
+        return pltpu.make_async_remote_copy(
+            src_ref=middle.at[k, pl.ds(pl.multiple_of(xh_ * 64, 64), 64), :],
+            dst_ref=pieces.at[k % 2, xh * 2 + xl],
+            send_sem=s5.at[k, dh],
+            recv_sem=r5.at[k % 2],
+            device_id=device(y, owner(k), core, z * 2 + xh_),
+            device_id_type=MESH,
+        )
+
+    def direct_part(row_):
+        return parts.at[SLOTS_DEV - 1, pl.ds(pl.multiple_of(row_ * 64, 64), 64), :]
+
+    def direct(dr):
+        row_ = (row + dr) % 8
+        return pltpu.make_async_remote_copy(
+            src_ref=direct_part(row_),
+            dst_ref=last.at[seg],
+            send_sem=s4.at[0 if dr else 1],
+            recv_sem=r4,
+            device_id=device(y, owner(SLOTS_DEV - 1), core, row_),
+            device_id_type=MESH,
+        )
+
+    def second(k):
+        with jax.named_scope(f"wait_stage#k={k}"):
+            pltpu.make_async_copy(stage.at[k], stage.at[k], r3.at[k]).wait()
+        acc = parts[k, pl.ds(pl.multiple_of(z * 128, 128), 128), :].astype(jnp.float32)
+        for n in range(3):
+            acc += stage[k, n].astype(jnp.float32)
+        middle[k] = acc.astype(jnp.bfloat16)
+        across(k, 1).start()
+
+        @pl.when(xl == owner(k))
+        def _():
+            pltpu.make_async_copy(
+                middle.at[k, pl.ds(pl.multiple_of(xh * 64, 64), 64), :],
+                pieces.at[k % 2, xh * 2 + xl],
+                r5.at[k % 2],
             ).start()
-        own = parts.at[k, pl.ds(pl.multiple_of(row * 64, 64), 64), :]
-
-        @pl.when(xl == owner)
+
+        @pl.when(xl != owner(k))
         def _():
-            pltpu.make_async_copy(own, pieces.at[k % 2, seg], r3.at[k % 2]).start()
-
-        @pl.when(xl != owner)
-        def _():
-            pltpu.make_async_remote_copy(
-                src_ref=own,
-                dst_ref=pieces.at[k % 2, seg],
-                send_sem=s3.at[k, 1],
-                recv_sem=r3.at[k % 2],
-                device_id=device(y, 1 - xl, core, row),
-                device_id_type=MESH,
-            ).start()
-
+            across(k, 0).start()
+
+    for q in ORDER:
+        send_fields(1, q)
     for k in range(SLOTS_DEV):
         slot(k)
-
-    for k in range(2):
-        pltpu.make_async_copy(pieces.at[k], pieces.at[k], r3.at[k]).wait()
-        acc = pieces[k, 0].astype(jnp.float32)
-        for n in range(1, 16):
-            acc += pieces[k, n].astype(jnp.float32)
+        if k:
+            second(k - 1)
+
+    def combine(k, src, count):
+        acc = src[0].astype(jnp.float32)
+        for n in range(1, count):
+            acc += src[n].astype(jnp.float32)
         out_k[k] = acc[:, :512]
         out_m[k] = acc[:, 512:]
+
+    def two_stage(k):
+        with jax.named_scope(f"wait_pieces#k={k}"):
+            pltpu.make_async_copy(pieces.at[k], pieces.at[k], r5.at[k]).wait()
+        combine(k, pieces.at[k], 4)
+
+    two_stage(0)
+
+    @pl.when(xl == owner(0))
+    def _():
+        two_stage(1)
+
+    @pl.when(xl != owner(0))
+    def _():
+        with jax.named_scope("wait_last"):
+            pltpu.make_async_copy(last, last, r4).wait()
+        combine(1, last, 16)
 
     for q in range(NCHUNK):
         gone = arrived.at[q, pl.ds(0, 60)]
@@ -272,17 +351,23 @@
         pltpu.make_async_copy(gone, gone, s2.at[k]).wait()
         halo(k, True).wait_send()
         halo(k, False).wait_send()
-        gone = parts.at[k, pl.ds(0, 448), :]
-        pltpu.make_async_copy(gone, gone, s3.at[k, 0]).wait()
-
-        @pl.when(xl != k // 2)
-        def _():
-            gone = parts.at[k, pl.ds(0, 64), :]
-            pltpu.make_async_copy(gone, gone, s3.at[k, 1]).wait()
+        if k < SLOTS_DEV - 1:
+            pltpu.make_async_copy(stage.at[k], stage.at[k], s3.at[k]).wait()
+            across(k, 1).wait_send()
+
+            @pl.when(xl != owner(k))
+            def _():
+                across(k, 0).wait_send()
+        else:
+            gone = parts.at[k, pl.ds(0, 448), :]
+            pltpu.make_async_copy(gone, gone, s4.at[0]).wait()
+
+            @pl.when(xl != owner(k))
+            def _():
+                direct(0).wait_send()
 
 
 def per_device(psi_sectors, stiff_blocks, mass_blocks, harmonic_table):
-    table = coefficients(harmonic_table, 64)
     anywhere = pl.BlockSpec(memory_space=pl.ANY)
     vmem = pl.BlockSpec(memory_space=pltpu.VMEM)
     bf16, f32 = jnp.bfloat16, jnp.float32
@@ -293,7 +378,7 @@
             jax.ShapeDtypeStruct((2, 64, 512), f32),
             jax.ShapeDtypeStruct((2, 64, 512), f32),
         ),
-        in_specs=[anywhere, anywhere, anywhere, vmem],
+        in_specs=[anywhere, anywhere, anywhere, pl.BlockSpec(memory_space=pltpu.SMEM)],
         out_specs=(vmem, vmem),
         scratch_shapes=[
             pltpu.VMEM((NCHUNK, 64, PIECE, M), bf16),
@@ -304,7 +389,10 @@
             pltpu.VMEM((CHUNK, 4 * M), bf16),
             pltpu.VMEM((2 * M, 4 * M), f32),
             pltpu.VMEM((SLOTS_DEV, 2 * M, 4 * M), bf16),
-            pltpu.VMEM((2, 16, 64, 4 * M), bf16),
+            pltpu.VMEM((SLOTS_DEV - 1, 3, 128, 4 * M), bf16),
+            pltpu.VMEM((SLOTS_DEV - 1, 128, 4 * M), bf16),
+            pltpu.VMEM((2, 4, 64, 4 * M), bf16),
+            pltpu.VMEM((16, 64, 4 * M), bf16),
             dma((2, NBAND)),
             dma((NCHUNK,)),
             dma((NCHUNK,)),
@@ -312,14 +400,18 @@
             dma((SLOTS_DEV, NCHUNK)),
             dma((SLOTS_DEV, 2)),
             dma((SLOTS_DEV, 2)),
-            dma((SLOTS_DEV, 2)),
+            dma((SLOTS_DEV - 1,)),
+            dma((SLOTS_DEV - 1,)),
+            dma((2,)),
+            dma,
+            dma((SLOTS_DEV - 1, 2)),
             dma((2,)),
         ],
         compiler_params=pltpu.CompilerParams(
             collective_id=0, has_side_effects=True, vmem_limit_bytes=60 * 1024 * 1024
         ),
         name="reduce_sectors",
-    )(psi_sectors, stiff_blocks, mass_blocks, table)
+    )(psi_sectors, stiff_blocks, mass_blocks, harmonic_table)
 
 
 def solution(mesh):

time: 205 us -> 145 us (0.71)
  the two profiles are of different devices: /device:TPU:26 before, /device:TPU:1 now
where the time goes in v2:
time: 145 us; the launch traced here: 143 us
  Pallas kernels  139 us (96%)
  local copies, waits for them, and re-layouts  3.34 us (2%)
    pallas_call x1, Pallas kernels, per_device(): pl.pallas_call(kernel, out_shape=(jax.ShapeDtypeStruct((2, 64, 512), f32)...  139 us
    unnamed x2, local copies, waits for them, and re-layouts  3.34 us

profile of v2, /device:TPU:1, one launch (start us, length us, event | category | flops | bytes accessed | tf_op | source)
XLA Modules:
  0.0 143.1 jit_solution(1975762515428836697)
XLA Ops:
  0.6 139.2 %reduce_sectors.1 = (f32[2,64,512]{2,1,0:T(8,128)}, f32[2,64,512]{2,1,0:T(8,128)}) custom-call(bf16[4,2048,256]{2,1,0:T(8,128)(2,1)} %psi.1, bf16[16,5,128,128]{3,2,1,0:T(8,128)(2,1)} %stiff.1, bf16[16,5,128,128]{3,2,1,0:T(8,128)(2,1)} %mass.1, s32[32]{0:T(128)} %table.1), custom_call_target="tpu_custom_call" | custom-call | tf_op jit(solution)/shard_map/reduce_sectors/pallas_call | solution.py:375
  139.8 1.7 %copy.8 = f32[2,64,512]{2,1,0:T(8,128)} copy(f32[2,64,512]{2,1,0:T(8,128)} %get-tuple-element.4) | data formatting | bytes 524288
  141.5 1.7 %copy.9 = f32[2,64,512]{2,1,0:T(8,128)} copy(f32[2,64,512]{2,1,0:T(8,128)} %get-tuple-element.5) | data formatting | bytes 524288

commit v3 on v2

--- a/solution.py
+++ b/solution.py
@@ -21,6 +21,7 @@
 SLOTS_DEV = 4
 ORDER = (3, 0, 1, 2)
 HALO = 256
+WIDE = 512
 SECTORS = 64
 SLOTS = 32
 SECTOR_OFFSETS = tuple(
@@ -47,8 +48,9 @@
 
 def kernel(
     psi, stiff, mass, table, out_k, out_m,
-    arrived, sent, fields, lift, bands, images, total, parts, stage, middle, pieces, last,
-    load_sem, s1, r1, s2, r2, sh, rh, s3, r3, s4, r4, s5, r5,
+    arrived, sent, fields, lift, bands, images, total, parts,
+    stiff_in, stiff_mid, stiff_end, mass_in, mass_mid, mass_end,
+    load_sem, s1, r1, s2, r2, sh, rh, sk1, rk1, sk2, rk2, sm1, rm1, sm2, rm2,
 ):
     sec = lax.axis_index("sector")
     row = lax.axis_index("row")
@@ -170,7 +172,10 @@
 
         with jax.named_scope(f"transform#q={q}"):
             lax.fori_loop(0, PIECE // TILE, transform, 0)
-        send_fields(0, q)
+        for k in (0, 1) if q in (3, 0) else (0,):
+            send_fields(k, q)
+    for k, q in ((2, 3), (2, 0), (1, 1), (1, 2)):
+        send_fields(k, q)
 
     for copy in loads:
         copy.wait()
@@ -213,14 +218,13 @@
             device_id_type=MESH,
         )
 
-    def slot(k):
-        if k + 2 < SLOTS_DEV:
-            for q in ORDER:
-                send_fields(k + 2, q)
+    def margins(k):
         arrival(k, 3)
         halo(k, True).start()
         arrival(k, 0)
         halo(k, False).start()
+
+    def slot(k):
         arrival(k, 1)
         with jax.named_scope(f"wait_low#k={k}"):
             halo(k, True).wait_recv()
@@ -236,112 +240,129 @@
         with jax.named_scope(f"process#k={k}#q=3"):
             process(k, 3, False)
         with jax.named_scope(f"narrow#k={k}"):
-            parts[k] = total[...].astype(jnp.bfloat16)
-        if k < SLOTS_DEV - 1:
-            for dz in (2, 1, 3):
-                column(k, dz).start()
-        else:
-            for dr in (4, 5, 3, 6, 2, 7, 1):
-                direct(dr).start()
-
-            @pl.when(xl == owner(k))
-            def _():
-                pltpu.make_async_copy(direct_part(row), last.at[seg], r4).start()
-
-            @pl.when(xl != owner(k))
-            def _():
-                direct(0).start()
-
-    def owner(k):
-        return (k // 2 + core) % 2
-
-    def column(k, dz):
-        z_ = (z + dz) % 4
-        return pltpu.make_async_remote_copy(
-            src_ref=parts.at[k, pl.ds(pl.multiple_of(z_ * 128, 128), 128), :],
-            dst_ref=stage.at[k, (3 - dz)],
-            send_sem=s3.at[k],
-            recv_sem=r3.at[k],
-            device_id=device(y, xl, core, z_ * 2 + xh),
-            device_id_type=MESH,
-        )
-
-    def across(k, dh):
-        xh_ = (xh + dh) % 2
-        return pltpu.make_async_remote_copy(
-            src_ref=middle.at[k, pl.ds(pl.multiple_of(xh_ * 64, 64), 64), :],
-            dst_ref=pieces.at[k % 2, xh * 2 + xl],
-            send_sem=s5.at[k, dh],
-            recv_sem=r5.at[k % 2],
-            device_id=device(y, owner(k), core, z * 2 + xh_),
-            device_id_type=MESH,
-        )
-
-    def direct_part(row_):
-        return parts.at[SLOTS_DEV - 1, pl.ds(pl.multiple_of(row_ * 64, 64), 64), :]
-
-    def direct(dr):
-        row_ = (row + dr) % 8
-        return pltpu.make_async_remote_copy(
-            src_ref=direct_part(row_),
-            dst_ref=last.at[seg],
-            send_sem=s4.at[0 if dr else 1],
-            recv_sem=r4,
-            device_id=device(y, owner(SLOTS_DEV - 1), core, row_),
-            device_id_type=MESH,
-        )
-
-    def second(k):
-        with jax.named_scope(f"wait_stage#k={k}"):
-            pltpu.make_async_copy(stage.at[k], stage.at[k], r3.at[k]).wait()
-        acc = parts[k, pl.ds(pl.multiple_of(z * 128, 128), 128), :].astype(jnp.float32)
-        for n in range(3):
-            acc += stage[k, n].astype(jnp.float32)
-        middle[k] = acc.astype(jnp.bfloat16)
-        across(k, 1).start()
+            parts[k] = total[...].astype(jnp.bfloat16).reshape(4, 2, 64, 2 * WIDE)
+        for dz in (2, 1, 3):
+            stiff_first(k, dz).start()
+        mass_first(k, 1).start()
 
         @pl.when(xl == owner(k))
         def _():
             pltpu.make_async_copy(
-                middle.at[k, pl.ds(pl.multiple_of(xh * 64, 64), 64), :],
-                pieces.at[k % 2, xh * 2 + xl],
-                r5.at[k % 2],
+                parts.at[k, :, xh, :, pl.ds(WIDE, WIDE)], mass_in.at[k % 2, place], rm1.at[k % 2]
             ).start()
 
         @pl.when(xl != owner(k))
         def _():
-            across(k, 0).start()
-
-    for q in ORDER:
-        send_fields(1, q)
-    for k in range(SLOTS_DEV):
-        slot(k)
-        if k:
-            second(k - 1)
-
-    def combine(k, src, count):
-        acc = src[0].astype(jnp.float32)
-        for n in range(1, count):
-            acc += src[n].astype(jnp.float32)
-        out_k[k] = acc[:, :512]
-        out_m[k] = acc[:, 512:]
-
-    def two_stage(k):
-        with jax.named_scope(f"wait_pieces#k={k}"):
-            pltpu.make_async_copy(pieces.at[k], pieces.at[k], r5.at[k]).wait()
-        combine(k, pieces.at[k], 4)
-
-    two_stage(0)
-
-    @pl.when(xl == owner(0))
-    def _():
-        two_stage(1)
-
-    @pl.when(xl != owner(0))
-    def _():
-        with jax.named_scope("wait_last"):
-            pltpu.make_async_copy(last, last, r4).wait()
-        combine(1, last, 16)
+            mass_first(k, 0).start()
+
+    place = xh * 2 + xl
+
+    def owner(k):
+        return (k // 2 + core) % 2
+
+    def stiff_first(k, dz):
+        z_ = (z + dz) % 4
+        return pltpu.make_async_remote_copy(
+            src_ref=parts.at[k, z_, :, :, pl.ds(0, WIDE)],
+            dst_ref=stiff_in.at[k, 3 - dz],
+            send_sem=sk1.at[k],
+            recv_sem=rk1.at[k],
+            device_id=device(y, xl, core, z_ * 2 + xh),
+            device_id_type=MESH,
+        )
+
+    def stiff_second(k, dh):
+        xh_ = (xh + dh) % 2
+        return pltpu.make_async_remote_copy(
+            src_ref=stiff_mid.at[k, xh_],
+            dst_ref=stiff_end.at[k % 2, place],
+            send_sem=sk2.at[k, dh],
+            recv_sem=rk2.at[k % 2],
+            device_id=device(y, owner(k), core, z * 2 + xh_),
+            device_id_type=MESH,
+        )
+
+    def mass_first(k, dh):
+        xh_ = (xh + dh) % 2
+        return pltpu.make_async_remote_copy(
+            src_ref=parts.at[k, :, xh_, :, pl.ds(WIDE, WIDE)],
+            dst_ref=mass_in.at[k % 2, place],
+            send_sem=sm1.at[k, dh],
+            recv_sem=rm1.at[k % 2],
+            device_id=device(y, owner(k), core, z * 2 + xh_),
+            device_id_type=MESH,
+        )
+
+    def mass_second(k, dz):
+        z_ = (z + dz) % 4
+        return pltpu.make_async_remote_copy(
+            src_ref=mass_mid.at[k % 2, z_],
+            dst_ref=mass_end.at[k % 2, 3 - dz],
+            send_sem=sm2.at[k % 2],
+            recv_sem=rm2.at[k % 2],
+            device_id=device(y, xl, core, z_ * 2 + xh),
+            device_id_type=MESH,
+        )
+
+    def whole(ref, sem):
+        pltpu.make_async_copy(ref, ref, sem).wait()
+
+    def second(k):
+        with jax.named_scope(f"wait_stiff#k={k}"):
+            whole(stiff_in.at[k], rk1.at[k])
+        acc = parts[k, z, :, :, pl.ds(0, WIDE)].astype(jnp.float32)
+        for n in range(3):
+            acc += stiff_in[k, n].astype(jnp.float32)
+        stiff_mid[k] = acc.astype(jnp.bfloat16)
+        stiff_second(k, 1).start()
+
+        @pl.when(xl == owner(k))
+        def _():
+            pltpu.make_async_copy(
+                stiff_mid.at[k, xh], stiff_end.at[k % 2, place], rk2.at[k % 2]
+            ).start()
+            with jax.named_scope(f"wait_mass#k={k}"):
+                whole(mass_in.at[k % 2], rm1.at[k % 2])
+            acc = mass_in[k % 2, 0].astype(jnp.float32)
+            for n in range(1, 4):
+                acc += mass_in[k % 2, n].astype(jnp.float32)
+            mass_mid[k % 2] = acc.astype(jnp.bfloat16)
+            for dz in (2, 1, 3):
+                mass_second(k, dz).start()
+
+        @pl.when(xl != owner(k))
+        def _():
+            stiff_second(k, 0).start()
+
+    margins(0)
+    margins(1)
+    slot(0)
+    for k, q in ((3, 3), (3, 0), (2, 1), (2, 2)):
+        send_fields(k, q)
+    margins(2)
+    slot(1)
+    for q in (1, 2):
+        send_fields(3, q)
+    second(0)
+    margins(3)
+    slot(2)
+    second(1)
+    slot(3)
+    second(2)
+    second(3)
+
+    for k in range(2):
+        with jax.named_scope(f"wait_end#k={k}"):
+            whole(stiff_end.at[k], rk2.at[k])
+            whole(mass_end.at[k], rm2.at[k])
+        acc = stiff_end[k, 0].astype(jnp.float32)
+        for n in range(1, 4):
+            acc += stiff_end[k, n].astype(jnp.float32)
+        out_k[k] = acc
+        acc = mass_mid[k, z].astype(jnp.float32)
+        for n in range(3):
+            acc += mass_end[k, n].astype(jnp.float32)
+        out_m[k] = acc
 
     for q in range(NCHUNK):
         gone = arrived.at[q, pl.ds(0, 60)]
@@ -351,20 +372,17 @@
         pltpu.make_async_copy(gone, gone, s2.at[k]).wait()
         halo(k, True).wait_send()
         halo(k, False).wait_send()
-        if k < SLOTS_DEV - 1:
-            pltpu.make_async_copy(stage.at[k], stage.at[k], s3.at[k]).wait()
-            across(k, 1).wait_send()
-
-            @pl.when(xl != owner(k))
-            def _():
-                across(k, 0).wait_send()
-        else:
-            gone = parts.at[k, pl.ds(0, 448), :]
-            pltpu.make_async_copy(gone, gone, s4.at[0]).wait()
-
-            @pl.when(xl != owner(k))
-            def _():
-                direct(0).wait_send()
+        whole(stiff_in.at[k], sk1.at[k])
+        stiff_second(k, 1).wait_send()
+        mass_first(k, 1).wait_send()
+
+        @pl.when(xl != owner(k))
+        def _():
+            stiff_second(k, 0).wait_send()
+            mass_first(k, 0).wait_send()
+
+    for k in range(2):
+        whole(mass_end.at[k], sm2.at[k])
 
 
 def per_device(psi_sectors, stiff_blocks, mass_blocks, harmonic_table):
@@ -388,11 +406,13 @@
             pltpu.VMEM((8, 2 * B, NBAND * B), bf16),
             pltpu.VMEM((CHUNK, 4 * M), bf16),
             pltpu.VMEM((2 * M, 4 * M), f32),
-            pltpu.VMEM((SLOTS_DEV, 2 * M, 4 * M), bf16),
-            pltpu.VMEM((SLOTS_DEV - 1, 3, 128, 4 * M), bf16),
-            pltpu.VMEM((SLOTS_DEV - 1, 128, 4 * M), bf16),
-            pltpu.VMEM((2, 4, 64, 4 * M), bf16),
-            pltpu.VMEM((16, 64, 4 * M), bf16),
+            pltpu.VMEM((SLOTS_DEV, 4, 2, 64, 2 * WIDE), bf16),
+            pltpu.VMEM((SLOTS_DEV, 3, 2, 64, WIDE), bf16),
+            pltpu.VMEM((SLOTS_DEV, 2, 64, WIDE), bf16),
+            pltpu.VMEM((2, 4, 64, WIDE), bf16),
+            pltpu.VMEM((2, 4, 4, 64, WIDE), bf16),
+            pltpu.VMEM((2, 4, 64, WIDE), bf16),
+            pltpu.VMEM((2, 3, 64, WIDE), bf16),
             dma((2, NBAND)),
             dma((NCHUNK,)),
             dma((NCHUNK,)),
@@ -400,11 +420,13 @@
             dma((SLOTS_DEV, NCHUNK)),
             dma((SLOTS_DEV, 2)),
             dma((SLOTS_DEV, 2)),
-            dma((SLOTS_DEV - 1,)),
-            dma((SLOTS_DEV - 1,)),
+            dma((SLOTS_DEV,)),
+            dma((SLOTS_DEV,)),
+            dma((SLOTS_DEV, 2)),
             dma((2,)),
-            dma,
-            dma((SLOTS_DEV - 1, 2)),
+            dma((SLOTS_DEV, 2)),
+            dma((2,)),
+            dma((2,)),
             dma((2,)),
         ],
         compiler_params=pltpu.CompilerParams(

time: 145 us -> 127 us (0.88); the launches traced: 143 us -> 127 us
  Pallas kernels: 139 us -> 123 us
    pallas_call x1, Pallas kernels: 139 us -> 123 us  [per_device(): pl.pallas_call(kernel, out_shape=(jax.ShapeDtypeStruct((2, 64, 512), f32)...]
where the time goes in v3:
time: 127 us
  Pallas kernels  123 us (97%)
  local copies, waits for them, and re-layouts  3.34 us (3%)
    pallas_call x1, Pallas kernels, per_device(): pl.pallas_call(kernel, out_shape=(jax.ShapeDtypeStruct((2, 64, 512), f32)...  123 us
    unnamed x2, local copies, waits for them, and re-layouts  3.34 us

profile of v3, /device:TPU:1, one launch (start us, length us, event | category | flops | bytes accessed | tf_op | source)
XLA Modules:
  0.0 126.7 jit_solution(4270100617128263316)
XLA Ops:
  0.6 122.7 %reduce_sectors.1 = (f32[2,64,512]{2,1,0:T(8,128)}, f32[2,64,512]{2,1,0:T(8,128)}) custom-call(bf16[4,2048,256]{2,1,0:T(8,128)(2,1)} %psi.1, bf16[16,5,128,128]{3,2,1,0:T(8,128)(2,1)} %stiff.1, bf16[16,5,128,128]{3,2,1,0:T(8,128)(2,1)} %mass.1, s32[32]{0:T(128)} %table.1), custom_call_target="tpu_custom_call" | custom-call | tf_op jit(solution)/shard_map/reduce_sectors/pallas_call | solution.py:393
  123.3 1.7 %copy.8 = f32[2,64,512]{2,1,0:T(8,128)} copy(f32[2,64,512]{2,1,0:T(8,128)} %get-tuple-element.4) | data formatting | bytes 524288
  125.0 1.7 %copy.9 = f32[2,64,512]{2,1,0:T(8,128)} copy(f32[2,64,512]{2,1,0:T(8,128)} %get-tuple-element.5) | data formatting | bytes 524288

commit v4 on v3

--- a/solution.py
+++ b/solution.py
@@ -47,9 +47,9 @@
 
 
 def kernel(
-    psi, stiff, mass, table, out_k, out_m,
-    arrived, sent, fields, lift, bands, images, total, parts,
-    stiff_in, stiff_mid, stiff_end, mass_in, mass_mid, mass_end,
+    psi, stiff, mass, table, out,
+    arrived, sent, fields, lift, bands, edges, images, total, parts,
+    stiff_in, stiff_mid, stiff_end, mass_in, mass_mid, mass_end, result, done,
     load_sem, s1, r1, s2, r2, sh, rh, sk1, rk1, sk2, rk2, sm1, rm1, sm2, rm2,
 ):
     sec = lax.axis_index("sector")
@@ -180,7 +180,29 @@
     for copy in loads:
         copy.wait()
 
-    def process(k, q, first):
+    blank = pl.ds(pl.multiple_of((1 - core) * (HALO + SEG), HALO), HALO)
+    for k in range(SLOTS_DEV):
+        fields[k, :, blank, :] = jnp.zeros((2, HALO, M), jnp.bfloat16)
+    near_block, far_block = core * 7, 1 + core * 5
+    for n, (block, lane) in enumerate(
+        ((near_block, B + core * 2 * B), (far_block, core * 4 * B), (near_block, core * 4 * B))
+    ):
+        for m in range(2):
+            piece = bands[block, pl.ds(m * B, B), pl.ds(pl.multiple_of(lane, B), B)]
+            edges[n, pl.ds(m * B, B), :] = piece.astype(jnp.float32).T.astype(jnp.bfloat16)
+
+    def project(rows, first):
+        for e in range(2):
+            part = lax.dot_general(
+                rows[e], images[...], (((0,), (0,)), ((), ())), preferred_element_type=jnp.float32
+            )
+            at = pl.ds(e * M, M)
+            if first:
+                total[at, :] = part
+            else:
+                total[at, :] += part
+
+    def process(k, q):
         for b in range(2):
             i = 2 * q + b
             for e in range(2):
@@ -189,56 +211,71 @@
                 w = w.astype(jnp.bfloat16)
                 images[pl.ds(b * B, B), pl.ds(e * M, M)] = w[:B]
                 images[pl.ds(b * B, B), pl.ds(2 * M + e * M, M)] = w[B:]
-        for e in range(2):
-            left = fields[k, e, pl.ds(HALO + q * CHUNK, CHUNK), :]
-            part = lax.dot_general(
-                left, images[...], (((0,), (0,)), ((), ())), preferred_element_type=jnp.float32
-            )
-            at = pl.ds(e * M, M)
-            if first:
-                total[at, :] = part
-            else:
-                total[at, :] += part
+        project(fields.at[k, :, pl.ds(HALO + q * CHUNK, CHUNK), :], False)
 
     def arrival(k, q):
         whole = fields.at[k, :, pl.ds(0, CHUNK), :]
         with jax.named_scope(f"wait_two#k={k}#q={q}"):
             pltpu.make_async_copy(whole, whole, r2.at[k, q]).wait()
 
-    def halo(k, up):
-        to = (seg + (1 if up else 15)) % 16
-        src, dst = (SEG, 0) if up else (HALO, HALO + SEG)
-        side = 0 if up else 1
+    edge_rows = pl.ds(pl.multiple_of(core * (HALO + SEG), HALO), HALO)
+
+    def halo(k):
+        to = (seg + 1 + 14 * core) % 16
+        mine = pl.ds(pl.multiple_of(SEG - core * (SEG - HALO), HALO), HALO)
         return pltpu.make_async_remote_copy(
-            src_ref=fields.at[k, :, pl.ds(src, HALO), :],
-            dst_ref=fields.at[k, :, pl.ds(dst, HALO), :],
-            send_sem=sh.at[k, side],
-            recv_sem=rh.at[k, side],
+            src_ref=fields.at[k, :, mine, :],
+            dst_ref=fields.at[k, :, edge_rows, :],
+            send_sem=sh.at[k],
+            recv_sem=rh.at[k],
             device_id=device(y, to % 2, core, to // 2),
             device_id_type=MESH,
         )
 
     def margins(k):
         arrival(k, 3)
-        halo(k, True).start()
+
+        @pl.when(core == 0)
+        def _():
+            halo(k).start()
+
         arrival(k, 0)
-        halo(k, False).start()
+
+        @pl.when(core == 1)
+        def _():
+            halo(k).start()
+
+    def boundary(k):
+        near = pl.ds(pl.multiple_of(HALO + core * 7 * B, B), B)
+        far = pl.ds(pl.multiple_of(HALO + B + core * 5 * B, B), B)
+        for e in range(2):
+            low = jnp.dot(edges[0], fields[k, e, near, :], preferred_element_type=jnp.float32)
+            low += jnp.dot(edges[1], fields[k, e, far, :], preferred_element_type=jnp.float32)
+            deep = jnp.dot(edges[2], fields[k, e, near, :], preferred_element_type=jnp.float32)
+            low, deep = low.astype(jnp.bfloat16), deep.astype(jnp.bfloat16)
+            at_low = pl.ds(pl.multiple_of((1 - core) * B, B), B)
+            at_deep = pl.ds(pl.multiple_of(core * B, B), B)
+            for m in range(2):
+                columns = pl.ds(m * 2 * M + e * M, M)
+                images[at_low, columns] = low[m * B : (m + 1) * B]
+                images[at_deep, columns] = deep[m * B : (m + 1) * B]
+        project(fields.at[k, :, edge_rows, :], True)
 
     def slot(k):
+        with jax.named_scope(f"wait_halo#k={k}"):
+            halo(k).wait_recv()
+        with jax.named_scope(f"boundary#k={k}"):
+            boundary(k)
         arrival(k, 1)
-        with jax.named_scope(f"wait_low#k={k}"):
-            halo(k, True).wait_recv()
         with jax.named_scope(f"process#k={k}#q=0"):
-            process(k, 0, True)
+            process(k, 0)
         arrival(k, 2)
         with jax.named_scope(f"process#k={k}#q=1"):
-            process(k, 1, False)
+            process(k, 1)
         with jax.named_scope(f"process#k={k}#q=2"):
-            process(k, 2, False)
-        with jax.named_scope(f"wait_high#k={k}"):
-            halo(k, False).wait_recv()
+            process(k, 2)
         with jax.named_scope(f"process#k={k}#q=3"):
-            process(k, 3, False)
+            process(k, 3)
         with jax.named_scope(f"narrow#k={k}"):
             parts[k] = total[...].astype(jnp.bfloat16).reshape(4, 2, 64, 2 * WIDE)
         for dz in (2, 1, 3):
@@ -346,8 +383,8 @@
     second(0)
     margins(3)
     slot(2)
+    slot(3)
     second(1)
-    slot(3)
     second(2)
     second(3)
 
@@ -358,20 +395,21 @@
         acc = stiff_end[k, 0].astype(jnp.float32)
         for n in range(1, 4):
             acc += stiff_end[k, n].astype(jnp.float32)
-        out_k[k] = acc
+        result[0, k] = acc
         acc = mass_mid[k, z].astype(jnp.float32)
         for n in range(3):
             acc += mass_end[k, n].astype(jnp.float32)
-        out_m[k] = acc
-
+        result[1, k] = acc
+
+    final = pltpu.make_async_copy(result, out, done)
+    final.start()
     for q in range(NCHUNK):
         gone = arrived.at[q, pl.ds(0, 60)]
         pltpu.make_async_copy(gone, gone, s1.at[q]).wait()
     for k in range(SLOTS_DEV):
         gone = sent.at[pl.ds(0, 4), pl.ds(0, 14)]
         pltpu.make_async_copy(gone, gone, s2.at[k]).wait()
-        halo(k, True).wait_send()
-        halo(k, False).wait_send()
+        halo(k).wait_send()
         whole(stiff_in.at[k], sk1.at[k])
         stiff_second(k, 1).wait_send()
         mass_first(k, 1).wait_send()
@@ -383,6 +421,7 @@
 
     for k in range(2):
         whole(mass_end.at[k], sm2.at[k])
+    final.wait()
 
 
 def per_device(psi_sectors, stiff_blocks, mass_blocks, harmonic_table):
@@ -390,20 +429,18 @@
     vmem = pl.BlockSpec(memory_space=pltpu.VMEM)
     bf16, f32 = jnp.bfloat16, jnp.float32
     dma = pltpu.SemaphoreType.DMA
-    return pl.pallas_call(
+    out = pl.pallas_call(
         kernel,
-        out_shape=(
-            jax.ShapeDtypeStruct((2, 64, 512), f32),
-            jax.ShapeDtypeStruct((2, 64, 512), f32),
-        ),
+        out_shape=jax.ShapeDtypeStruct((2, 2, 64, 512), f32),
         in_specs=[anywhere, anywhere, anywhere, pl.BlockSpec(memory_space=pltpu.SMEM)],
-        out_specs=(vmem, vmem),
+        out_specs=pl.BlockSpec(memory_space=pl.ANY),
         scratch_shapes=[
             pltpu.VMEM((NCHUNK, 64, PIECE, M), bf16),
             pltpu.VMEM((NCHUNK, 64, PIECE, M), bf16),
             pltpu.VMEM((SLOTS_DEV, 2, SEG + 2 * HALO, M), bf16),
             pltpu.VMEM((2, 1024, 1024), bf16),
             pltpu.VMEM((8, 2 * B, NBAND * B), bf16),
+            pltpu.VMEM((3, 2 * B, B), bf16),
             pltpu.VMEM((CHUNK, 4 * M), bf16),
             pltpu.VMEM((2 * M, 4 * M), f32),
             pltpu.VMEM((SLOTS_DEV, 4, 2, 64, 2 * WIDE), bf16),
@@ -413,13 +450,15 @@
             pltpu.VMEM((2, 4, 4, 64, WIDE), bf16),
             pltpu.VMEM((2, 4, 64, WIDE), bf16),
             pltpu.VMEM((2, 3, 64, WIDE), bf16),
+            pltpu.VMEM((2, 2, 64, WIDE), f32),
+            dma,
             dma((2, NBAND)),
             dma((NCHUNK,)),
             dma((NCHUNK,)),
             dma((SLOTS_DEV,)),
             dma((SLOTS_DEV, NCHUNK)),
-            dma((SLOTS_DEV, 2)),
-            dma((SLOTS_DEV, 2)),
+            dma((SLOTS_DEV,)),
+            dma((SLOTS_DEV,)),
             dma((SLOTS_DEV,)),
             dma((SLOTS_DEV,)),
             dma((SLOTS_DEV, 2)),
@@ -430,10 +469,11 @@
             dma((2,)),
         ],
         compiler_params=pltpu.CompilerParams(
-            collective_id=0, has_side_effects=True, vmem_limit_bytes=60 * 1024 * 1024
+            collective_id=0, has_side_effects=True, vmem_limit_bytes=52 * 1024 * 1024
         ),
         name="reduce_sectors",
     )(psi_sectors, stiff_blocks, mass_blocks, harmonic_table)
+    return out[0], out[1]
 
 
 def solution(mesh):

time: 127 us -> 122 us (0.961)
  Pallas kernels: 123 us -> 119 us
  local copies, waits for them, and re-layouts: 3.34 us -> 1.47 us
    pallas_call x1, Pallas kernels: 123 us -> 119 us  [per_device(): pl.pallas_call(kernel, out_shape=jax.ShapeDtypeStruct((2, 2, 64, 512), f3...]
    unnamed x2, local copies, waits for them, and re-layouts: 3.34 us -> 0.65 us
where the time goes in v4:
time: 122 us; the launch traced here: 121 us
  Pallas kernels  119 us (98%)
  local copies, waits for them, and re-layouts  1.47 us (1%)
    pallas_call x1, Pallas kernels, per_device(): pl.pallas_call(kernel, out_shape=jax.ShapeDtypeStruct((2, 2, 64, 512), f3...  119 us

profile of v4, /device:TPU:1, one launch (start us, length us, event | category | flops | bytes accessed | tf_op | source)
XLA Modules:
  0.0 121.4 jit_solution(6729009571244431245)
XLA Ops:
  0.6 0.0 copy-start
  0.6 0.6 copy-done
  1.3 119.3 %reduce_sectors.1 = f32[2,2,64,512]{3,2,1,0:T(8,128)S(1)} custom-call(bf16[4,2048,256]{2,1,0:T(8,128)(2,1)} %psi.1, bf16[16,5,128,128]{3,2,1,0:T(8,128)(2,1)} %stiff.1, bf16[16,5,128,128]{3,2,1,0:T(8,128)(2,1)} %mass.1, s32[32]{0:T(128)S(1)} %copy-done), custom_call_target="tpu_custom_call" | custom-call | tf_op jit(solution)/shard_map/reduce_sectors/pallas_call | solution.py:432
  120.6 0.8 slice_bitcast_fusion
Async XLA Ops:
  0.6 0.7 copy-start

commit v5 on v4

--- a/solution.py
+++ b/solution.py
@@ -138,21 +138,38 @@
     with jax.named_scope("spread"):
         lax.fori_loop(0, 4, spread, 0)
 
-    def send_fields(k, q):
-        mine = pl.ds(pl.multiple_of(HALO + q * CHUNK + turn * PIECE, PIECE), PIECE)
+    def mine(q):
+        return pl.ds(pl.multiple_of(HALO + q * CHUNK + turn * PIECE, PIECE), PIECE)
+
+    def send_fields(k, chunk):
         for dy, dc in OWNER_OFFSETS:
             y_, core_ = (y + dy) % 4, (core + dc) % 2
+            q = chunk(core_)
             pltpu.make_async_remote_copy(
                 src_ref=sent.at[q, pl.ds(k * 16 + (y_ * 2 + core_) * 2, 2)],
-                dst_ref=fields.at[k, :, mine, :],
+                dst_ref=fields.at[k, :, mine(q), :],
                 send_sem=s2.at[k],
                 recv_sem=r2.at[k, q],
                 device_id=device(y_, xl, core_, row),
                 device_id_type=MESH,
             ).start()
+        q = chunk(core)
         pltpu.make_async_copy(
-            sent.at[q, pl.ds(k * 16 + turn * 2, 2)], fields.at[k, :, mine, :], r2.at[k, q]
+            sent.at[q, pl.ds(k * 16 + turn * 2, 2)], fields.at[k, :, mine(q), :], r2.at[k, q]
         ).start()
+
+    def first_chunk(core_):
+        return 3 * (1 - core_)
+
+    def second_chunk(core_):
+        return 3 * core_
+
+    def send_slot(k):
+        send_fields(k, second_chunk)
+        if k + 1 < SLOTS_DEV:
+            send_fields(k + 1, first_chunk)
+        send_fields(k, lambda core_: 1)
+        send_fields(k, lambda core_: 2)
 
     for q in ORDER:
         with jax.named_scope(f"wait_one#q={q}"):
@@ -172,10 +189,10 @@
 
         with jax.named_scope(f"transform#q={q}"):
             lax.fori_loop(0, PIECE // TILE, transform, 0)
-        for k in (0, 1) if q in (3, 0) else (0,):
-            send_fields(k, q)
-    for k, q in ((2, 3), (2, 0), (1, 1), (1, 2)):
-        send_fields(k, q)
+        send_fields(0, lambda core_: q)
+        if q == 0:
+            send_fields(1, first_chunk)
+    send_slot(1)
 
     for copy in loads:
         copy.wait()
@@ -215,7 +232,7 @@
 
     def arrival(k, q):
         whole = fields.at[k, :, pl.ds(0, CHUNK), :]
-        with jax.named_scope(f"wait_two#k={k}#q={q}"):
+        with jax.named_scope(f"wait_two#k={k}"):
             pltpu.make_async_copy(whole, whole, r2.at[k, q]).wait()
 
     edge_rows = pl.ds(pl.multiple_of(core * (HALO + SEG), HALO), HALO)
@@ -232,18 +249,9 @@
             device_id_type=MESH,
         )
 
-    def margins(k):
-        arrival(k, 3)
-
-        @pl.when(core == 0)
-        def _():
-            halo(k).start()
-
-        arrival(k, 0)
-
-        @pl.when(core == 1)
-        def _():
-            halo(k).start()
+    def pass_on(k):
+        arrival(k, first_chunk(core))
+        halo(k).start()
 
     def boundary(k):
         near = pl.ds(pl.multiple_of(HALO + core * 7 * B, B), B)
@@ -262,6 +270,9 @@
         project(fields.at[k, :, edge_rows, :], True)
 
     def slot(k):
+        arrival(k, second_chunk(core))
+        if k + 1 < SLOTS_DEV:
+            pass_on(k + 1)
         with jax.named_scope(f"wait_halo#k={k}"):
             halo(k).wait_recv()
         with jax.named_scope(f"boundary#k={k}"):
@@ -371,22 +382,17 @@
         def _():
             stiff_second(k, 0).start()
 
-    margins(0)
-    margins(1)
-    slot(0)
-    for k, q in ((3, 3), (3, 0), (2, 1), (2, 2)):
-        send_fields(k, q)
-    margins(2)
-    slot(1)
-    for q in (1, 2):
-        send_fields(3, q)
-    second(0)
-    margins(3)
-    slot(2)
-    slot(3)
-    second(1)
-    second(2)
-    second(3)
+    for k in range(SLOTS_DEV):
+        if k + 2 < SLOTS_DEV:
+            send_slot(k + 2)
+        if k == 0:
+            pass_on(0)
+        slot(k)
+        if k in (1, 2):
+            second(k - 1)
+    for k in range(SLOTS_DEV):
+        if k + 1 not in (1, 2):
+            second(k)
 
     for k in range(2):
         with jax.named_scope(f"wait_end#k={k}"):

time: 122 us -> 119 us (0.975)
  Pallas kernels: 119 us -> 117 us
    pallas_call x1, Pallas kernels: 119 us -> 117 us  [per_device(): pl.pallas_call(kernel, out_shape=jax.ShapeDtypeStruct((2, 2, 64, 512), f3...]
where the time goes in v5:
time: 119 us
  Pallas kernels  117 us (98%)
  local copies, waits for them, and re-layouts  1.47 us (1%)
    pallas_call x1, Pallas kernels, per_device(): pl.pallas_call(kernel, out_shape=jax.ShapeDtypeStruct((2, 2, 64, 512), f3...  117 us

profile of v5, /device:TPU:1, one launch (start us, length us, event | category | flops | bytes accessed | tf_op | source)
XLA Modules:
  0.0 119.1 jit_solution(3719755860698053656)
XLA Ops:
  0.6 0.0 copy-start
  0.6 0.6 copy-done
  1.3 117.0 %reduce_sectors.1 = f32[2,2,64,512]{3,2,1,0:T(8,128)S(1)} custom-call(bf16[4,2048,256]{2,1,0:T(8,128)(2,1)} %psi.1, bf16[16,5,128,128]{3,2,1,0:T(8,128)(2,1)} %stiff.1, bf16[16,5,128,128]{3,2,1,0:T(8,128)(2,1)} %mass.1, s32[32]{0:T(128)S(1)} %copy-done), custom_call_target="tpu_custom_call" | custom-call | tf_op jit(solution)/shard_map/reduce_sectors/pallas_call | solution.py:438
  118.3 0.8 slice_bitcast_fusion
Async XLA Ops:
  0.6 0.7 copy-start

commit v6 on v5

--- a/solution.py
+++ b/solution.py
@@ -19,6 +19,7 @@
 PIECE = 32
 TILE = 16
 SLOTS_DEV = 4
+LAST = SLOTS_DEV - 1
 ORDER = (3, 0, 1, 2)
 HALO = 256
 WIDE = 512
@@ -50,7 +51,7 @@
     psi, stiff, mass, table, out,
     arrived, sent, fields, lift, bands, edges, images, total, parts,
     stiff_in, stiff_mid, stiff_end, mass_in, mass_mid, mass_end, result, done,
-    load_sem, s1, r1, s2, r2, sh, rh, sk1, rk1, sk2, rk2, sm1, rm1, sm2, rm2,
+    load_sem, s1, r1, s2, r2, rc, sh, rh, sk1, rk1, sk2, rk2, sm1, rm1, sm2, rm2,
 ):
     sec = lax.axis_index("sector")
     row = lax.axis_index("row")
@@ -168,8 +169,26 @@
         send_fields(k, second_chunk)
         if k + 1 < SLOTS_DEV:
             send_fields(k + 1, first_chunk)
-        send_fields(k, lambda core_: 1)
-        send_fields(k, lambda core_: 2)
+        for step in range(2):
+            for q in (1, 2):
+                send_component(k, q, step)
+
+    def send_component(k, q, step):
+        for dy, dc in OWNER_OFFSETS:
+            y_, core_ = (y + dy) % 4, (core + dc) % 2
+            e = (step + core_) % 2
+            pltpu.make_async_remote_copy(
+                src_ref=sent.at[q, k * 16 + (y_ * 2 + core_) * 2 + e],
+                dst_ref=fields.at[k, e, mine(q), :],
+                send_sem=s2.at[k],
+                recv_sem=rc.at[k, q - 1, step],
+                device_id=device(y_, xl, core_, row),
+                device_id_type=MESH,
+            ).start()
+        e = (step + core) % 2
+        pltpu.make_async_copy(
+            sent.at[q, k * 16 + turn * 2 + e], fields.at[k, e, mine(q), :], rc.at[k, q - 1, step]
+        ).start()
 
     for q in ORDER:
         with jax.named_scope(f"wait_one#q={q}"):
@@ -189,7 +208,11 @@
 
         with jax.named_scope(f"transform#q={q}"):
             lax.fori_loop(0, PIECE // TILE, transform, 0)
-        send_fields(0, lambda core_: q)
+        if q in (1, 2):
+            for step in range(2):
+                send_component(0, q, step)
+        else:
+            send_fields(0, lambda core_: q)
         if q == 0:
             send_fields(1, first_chunk)
     send_slot(1)
@@ -208,27 +231,19 @@
             piece = bands[block, pl.ds(m * B, B), pl.ds(pl.multiple_of(lane, B), B)]
             edges[n, pl.ds(m * B, B), :] = piece.astype(jnp.float32).T.astype(jnp.bfloat16)
 
+    def across_rows(left, right):
+        return lax.dot_general(
+            left, right, (((0,), (0,)), ((), ())), preferred_element_type=jnp.float32
+        )
+
     def project(rows, first):
         for e in range(2):
-            part = lax.dot_general(
-                rows[e], images[...], (((0,), (0,)), ((), ())), preferred_element_type=jnp.float32
-            )
+            part = across_rows(rows[e], images[pl.ds(0, CHUNK), :])
             at = pl.ds(e * M, M)
             if first:
                 total[at, :] = part
             else:
                 total[at, :] += part
-
-    def process(k, q):
-        for b in range(2):
-            i = 2 * q + b
-            for e in range(2):
-                window = fields[k, e, pl.ds(i * B, NBAND * B), :]
-                w = jnp.dot(bands[i], window, preferred_element_type=jnp.float32)
-                w = w.astype(jnp.bfloat16)
-                images[pl.ds(b * B, B), pl.ds(e * M, M)] = w[:B]
-                images[pl.ds(b * B, B), pl.ds(2 * M + e * M, M)] = w[B:]
-        project(fields.at[k, :, pl.ds(HALO + q * CHUNK, CHUNK), :], False)
 
     def arrival(k, q):
         whole = fields.at[k, :, pl.ds(0, CHUNK), :]
@@ -270,54 +285,124 @@
         project(fields.at[k, :, edge_rows, :], True)
 
     def slot(k):
+        own, other = core, 1 - core
+
+        def lanes(start, e):
+            return pl.ds(pl.multiple_of(start + e * M, M), M)
+
+        def widen(q, e):
+            for b in range(2):
+                i = 2 * q + b
+                window = fields[k, e, pl.ds(i * B, NBAND * B), :]
+                w = jnp.dot(bands[i], window, preferred_element_type=jnp.float32)
+                w = w.astype(jnp.bfloat16)
+                images[pl.ds(i * B, B), lanes(0, e)] = w[:B]
+                images[pl.ds(i * B, B), lanes(2 * M, e)] = w[B:]
+
+        def add(chunks, e, columns):
+            start, size = chunks[0] * CHUNK, len(chunks) * CHUNK
+            left = fields[k, e, pl.ds(HALO + start, size), :]
+            for at in columns:
+                total[lanes(0, e), at] += across_rows(left, images[pl.ds(start, size), at])
+
+        def component(q, step):
+            whole(fields.at[k, 0, pl.ds(0, CHUNK), :], rc.at[k, q - 1, step])
+
+        def first_half(*chunks):
+            for q in chunks:
+                widen(q, own)
+            add(chunks, own, (lanes(0, own), lanes(2 * M, own)))
+
+        def second_half(*chunks):
+            for q in chunks:
+                widen(q, other)
+            add(chunks, own, (lanes(0, other), lanes(2 * M, other)))
+            add(chunks, other, (pl.ds(0, 4 * M),))
+
+        def narrow(e, at, width):
+            parts[k, pl.ds(2 * e, 2), :, :, at] = (
+                total[lanes(0, e), at].astype(jnp.bfloat16).reshape(2, 2, 64, width)
+            )
+
         arrival(k, second_chunk(core))
-        if k + 1 < SLOTS_DEV:
+        if k < LAST:
             pass_on(k + 1)
-        with jax.named_scope(f"wait_halo#k={k}"):
-            halo(k).wait_recv()
-        with jax.named_scope(f"boundary#k={k}"):
-            boundary(k)
-        arrival(k, 1)
-        with jax.named_scope(f"process#k={k}#q=0"):
-            process(k, 0)
-        arrival(k, 2)
-        with jax.named_scope(f"process#k={k}#q=1"):
-            process(k, 1)
-        with jax.named_scope(f"process#k={k}#q=2"):
-            process(k, 2)
-        with jax.named_scope(f"process#k={k}#q=3"):
-            process(k, 3)
-        with jax.named_scope(f"narrow#k={k}"):
-            parts[k] = total[...].astype(jnp.bfloat16).reshape(4, 2, 64, 2 * WIDE)
-        for dz in (2, 1, 3):
-            stiff_first(k, dz).start()
-        mass_first(k, 1).start()
-
-        @pl.when(xl == owner(k))
-        def _():
-            pltpu.make_async_copy(
-                parts.at[k, :, xh, :, pl.ds(WIDE, WIDE)], mass_in.at[k % 2, place], rm1.at[k % 2]
-            ).start()
-
-        @pl.when(xl != owner(k))
-        def _():
-            mass_first(k, 0).start()
+        halo(k).wait_recv()
+        boundary(k)
+        with jax.named_scope(f"component#k={k}#q=1#n=0"):
+            component(1, 0)
+        first_half(0)
+        with jax.named_scope(f"component#k={k}#q=2#n=0"):
+            component(2, 0)
+        with jax.named_scope(f"first_half#k={k}"):
+            first_half(1, 2, 3)
+            for m in range(2):
+                narrow(own, lanes(m * 2 * M, own), M)
+        send_sums(k, ((own, own),))
+        with jax.named_scope(f"component#k={k}#q=1#n=1"):
+            component(1, 1)
+        second_half(0)
+        with jax.named_scope(f"component#k={k}#q=2#n=1"):
+            component(2, 1)
+        with jax.named_scope(f"second_half#k={k}"):
+            second_half(1, 2, 3)
+            for m in range(2):
+                narrow(own, lanes(m * 2 * M, other), M)
+            narrow(other, pl.ds(0, 4 * M), 4 * M)
+        send_sums(k, ((own, other), (other, None)))
+
+    def send_sums(k, blocks):
+        def lanes(start, e):
+            if e is None:
+                return pl.ds(start, WIDE)
+            return pl.ds(pl.multiple_of(start + e * M, M), M)
+
+        for rows_e, cols_e in blocks:
+            for dz in (2, 1, 3):
+                z_ = (z + dz) % 4
+
+                @pl.when(z_ // 2 == rows_e)
+                def _():
+                    pltpu.make_async_remote_copy(
+                        src_ref=parts.at[k, z_, :, :, lanes(0, cols_e)],
+                        dst_ref=stiff_in.at[k, 3 - dz, :, :, lanes(0, cols_e)],
+                        send_sem=sk1.at[k],
+                        recv_sem=rk1.at[k],
+                        device_id=device(y, xl, core, z_ * 2 + xh),
+                        device_id_type=MESH,
+                    ).start()
+
+            planes = pl.ds(2 * rows_e, 2)
+
+            def to_owner(dh):
+                xh_ = (xh + dh) % 2
+                return pltpu.make_async_remote_copy(
+                    src_ref=parts.at[k, planes, xh_, :, lanes(WIDE, cols_e)],
+                    dst_ref=mass_in.at[k % 2, place, planes, :, lanes(0, cols_e)],
+                    send_sem=sm1.at[k, dh],
+                    recv_sem=rm1.at[k % 2],
+                    device_id=device(y, owner(k), core, z * 2 + xh_),
+                    device_id_type=MESH,
+                )
+
+            to_owner(1).start()
+
+            @pl.when(xl == owner(k))
+            def _():
+                pltpu.make_async_copy(
+                    parts.at[k, planes, xh, :, lanes(WIDE, cols_e)],
+                    mass_in.at[k % 2, place, planes, :, lanes(0, cols_e)],
+                    rm1.at[k % 2],
+                ).start()
+
+            @pl.when(xl != owner(k))
+            def _():
+                to_owner(0).start()
 
     place = xh * 2 + xl
 
     def owner(k):
         return (k // 2 + core) % 2
-
-    def stiff_first(k, dz):
-        z_ = (z + dz) % 4
-        return pltpu.make_async_remote_copy(
-            src_ref=parts.at[k, z_, :, :, pl.ds(0, WIDE)],
-            dst_ref=stiff_in.at[k, 3 - dz],
-            send_sem=sk1.at[k],
-            recv_sem=rk1.at[k],
-            device_id=device(y, xl, core, z_ * 2 + xh),
-            device_id_type=MESH,
-        )
 
     def stiff_second(k, dh):
         xh_ = (xh + dh) % 2
@@ -447,7 +532,7 @@
             pltpu.VMEM((2, 1024, 1024), bf16),
             pltpu.VMEM((8, 2 * B, NBAND * B), bf16),
             pltpu.VMEM((3, 2 * B, B), bf16),
-            pltpu.VMEM((CHUNK, 4 * M), bf16),
+            pltpu.VMEM((SEG, 4 * M), bf16),
             pltpu.VMEM((2 * M, 4 * M), f32),
             pltpu.VMEM((SLOTS_DEV, 4, 2, 64, 2 * WIDE), bf16),
             pltpu.VMEM((SLOTS_DEV, 3, 2, 64, WIDE), bf16),
@@ -463,6 +548,7 @@
             dma((NCHUNK,)),
             dma((SLOTS_DEV,)),
             dma((SLOTS_DEV, NCHUNK)),
+            dma((SLOTS_DEV, 2, 2)),
             dma((SLOTS_DEV,)),
             dma((SLOTS_DEV,)),
             dma((SLOTS_DEV,)),

time: 119 us -> 117 us (0.983)
  Pallas kernels: 117 us -> 115 us
    pallas_call x1, Pallas kernels: 117 us -> 115 us  [per_device(): pl.pallas_call(kernel, out_shape=jax.ShapeDtypeStruct((2, 2, 64, 512), f3...]
where the time goes in v6:
time: 117 us
  Pallas kernels  115 us (98%)
  local copies, waits for them, and re-layouts  1.47 us (1%)
    pallas_call x1, Pallas kernels, per_device(): pl.pallas_call(kernel, out_shape=jax.ShapeDtypeStruct((2, 2, 64, 512), f3...  115 us

profile of v6, /device:TPU:1, one launch (start us, length us, event | category | flops | bytes accessed | tf_op | source)
XLA Modules:
  0.0 116.8 jit_solution(13133479925652364731)
XLA Ops:
  0.6 0.0 copy-start
  0.6 0.6 copy-done
  1.3 114.7 %reduce_sectors.1 = f32[2,2,64,512]{3,2,1,0:T(8,128)S(1)} custom-call(bf16[4,2048,256]{2,1,0:T(8,128)(2,1)} %psi.1, bf16[16,5,128,128]{3,2,1,0:T(8,128)(2,1)} %stiff.1, bf16[16,5,128,128]{3,2,1,0:T(8,128)(2,1)} %mass.1, s32[32]{0:T(128)S(1)} %copy-done), custom_call_target="tpu_custom_call" | custom-call | tf_op jit(solution)/shard_map/reduce_sectors/pallas_call | solution.py:523
  116.0 0.8 slice_bitcast_fusion
Async XLA Ops:
  0.6 0.7 copy-start

commit v7 on v6

--- a/solution.py
+++ b/solution.py
@@ -48,9 +48,9 @@
 
 
 def kernel(
-    psi, stiff, mass, table, out,
+    psi, stiff, mass, table_in, out,
     arrived, sent, fields, lift, bands, edges, images, total, parts,
-    stiff_in, stiff_mid, stiff_end, mass_in, mass_mid, mass_end, result, done,
+    stiff_in, stiff_mid, stiff_end, mass_in, mass_mid, mass_end, table, table_sem,
     load_sem, s1, r1, s2, r2, rc, sh, rh, sk1, rk1, sk2, rk2, sm1, rm1, sm2, rm2,
 ):
     sec = lax.axis_index("sector")
@@ -63,6 +63,23 @@
     def device(y_, xl_, core_, row_):
         return {"sector": y_ * 4 + xl_ * 2 + core_, "row": row_}
 
+    barrier = pltpu.get_barrier_semaphore()
+    count = 0
+    for dy, dx, dc in SECTOR_OFFSETS:
+        pl.semaphore_signal(
+            barrier, inc=1, device_id_type=MESH,
+            device_id=device((y + dy) % 4, (xl + dx) % 2, (core + dc) % 2, row),
+        )
+        count += 1
+    for dr in range(1, 8):
+        for dx in range(2):
+            pl.semaphore_signal(
+                barrier, inc=1, device_id_type=MESH,
+                device_id=device(y, (xl + dx) % 2, core, (row + dr) % 8),
+            )
+            count += 1
+    table_copy = pltpu.make_async_copy(table_in, table, table_sem)
+    table_copy.start()
     loads = []
     for m, src in enumerate((stiff, mass)):
         for k in range(NBAND):
@@ -74,21 +91,6 @@
             copy.start()
             loads.append(copy)
 
-    barrier = pltpu.get_barrier_semaphore()
-    count = 0
-    for dy, dx, dc in SECTOR_OFFSETS:
-        pl.semaphore_signal(
-            barrier, inc=1, device_id_type=MESH,
-            device_id=device((y + dy) % 4, (xl + dx) % 2, (core + dc) % 2, row),
-        )
-        count += 1
-    for dr in range(1, 8):
-        for dx in range(2):
-            pl.semaphore_signal(
-                barrier, inc=1, device_id_type=MESH,
-                device_id=device(y, (xl + dx) % 2, core, (row + dr) % 8),
-            )
-            count += 1
     with jax.named_scope("barrier"):
         pl.semaphore_wait(barrier, count)
 
@@ -110,6 +112,7 @@
             psi.at[:, rows_of(xl, turn, q), :], arrived.at[q, pl.ds(sec * 4, 4)], r1.at[q]
         ).start()
 
+    table_copy.wait()
     coef = coefficients(table)
     coef_hi = coef.astype(jnp.bfloat16)
     coef_lo = (coef - coef_hi.astype(jnp.float32)).astype(jnp.bfloat16)
@@ -317,7 +320,6 @@
             for q in chunks:
                 widen(q, other)
             add(chunks, own, (lanes(0, other), lanes(2 * M, other)))
-            add(chunks, other, (pl.ds(0, 4 * M),))
 
         def narrow(e, at, width):
             parts[k, pl.ds(2 * e, 2), :, :, at] = (
@@ -342,14 +344,18 @@
         with jax.named_scope(f"component#k={k}#q=1#n=1"):
             component(1, 1)
         second_half(0)
+        add((0,), other, (pl.ds(0, 4 * M),))
         with jax.named_scope(f"component#k={k}#q=2#n=1"):
             component(2, 1)
         with jax.named_scope(f"second_half#k={k}"):
             second_half(1, 2, 3)
             for m in range(2):
                 narrow(own, lanes(m * 2 * M, other), M)
+        send_sums(k, ((own, other),))
+        with jax.named_scope(f"third_part#k={k}"):
+            add((1, 2, 3), other, (pl.ds(0, 4 * M),))
             narrow(other, pl.ds(0, 4 * M), 4 * M)
-        send_sums(k, ((own, other), (other, None)))
+        send_sums(k, ((other, None),))
 
     def send_sums(k, blocks):
         def lanes(start, e):
@@ -358,6 +364,33 @@
             return pl.ds(pl.multiple_of(start + e * M, M), M)
 
         for rows_e, cols_e in blocks:
+            planes = pl.ds(2 * rows_e, 2)
+
+            def to_owner(dh):
+                xh_ = (xh + dh) % 2
+                return pltpu.make_async_remote_copy(
+                    src_ref=parts.at[k, planes, xh_, :, lanes(WIDE, cols_e)],
+                    dst_ref=mass_in.at[k % 2, place, planes, :, lanes(0, cols_e)],
+                    send_sem=sm1.at[k, dh],
+                    recv_sem=rm1.at[k % 2],
+                    device_id=device(y, owner(k), core, z * 2 + xh_),
+                    device_id_type=MESH,
+                )
+
+            to_owner(1).start()
+
+            @pl.when(xl == owner(k))
+            def _():
+                pltpu.make_async_copy(
+                    parts.at[k, planes, xh, :, lanes(WIDE, cols_e)],
+                    mass_in.at[k % 2, place, planes, :, lanes(0, cols_e)],
+                    rm1.at[k % 2],
+                ).start()
+
+            @pl.when(xl != owner(k))
+            def _():
+                to_owner(0).start()
+
             for dz in (2, 1, 3):
                 z_ = (z + dz) % 4
 
@@ -371,33 +404,6 @@
                         device_id=device(y, xl, core, z_ * 2 + xh),
                         device_id_type=MESH,
                     ).start()
-
-            planes = pl.ds(2 * rows_e, 2)
-
-            def to_owner(dh):
-                xh_ = (xh + dh) % 2
-                return pltpu.make_async_remote_copy(
-                    src_ref=parts.at[k, planes, xh_, :, lanes(WIDE, cols_e)],
-                    dst_ref=mass_in.at[k % 2, place, planes, :, lanes(0, cols_e)],
-                    send_sem=sm1.at[k, dh],
-                    recv_sem=rm1.at[k % 2],
-                    device_id=device(y, owner(k), core, z * 2 + xh_),
-                    device_id_type=MESH,
-                )
-
-            to_owner(1).start()
-
-            @pl.when(xl == owner(k))
-            def _():
-                pltpu.make_async_copy(
-                    parts.at[k, planes, xh, :, lanes(WIDE, cols_e)],
-                    mass_in.at[k % 2, place, planes, :, lanes(0, cols_e)],
-                    rm1.at[k % 2],
-                ).start()
-
-            @pl.when(xl != owner(k))
-            def _():
-                to_owner(0).start()
 
     place = xh * 2 + xl
 
@@ -479,21 +485,6 @@
         if k + 1 not in (1, 2):
             second(k)
 
-    for k in range(2):
-        with jax.named_scope(f"wait_end#k={k}"):
-            whole(stiff_end.at[k], rk2.at[k])
-            whole(mass_end.at[k], rm2.at[k])
-        acc = stiff_end[k, 0].astype(jnp.float32)
-        for n in range(1, 4):
-            acc += stiff_end[k, n].astype(jnp.float32)
-        result[0, k] = acc
-        acc = mass_mid[k, z].astype(jnp.float32)
-        for n in range(3):
-            acc += mass_end[k, n].astype(jnp.float32)
-        result[1, k] = acc
-
-    final = pltpu.make_async_copy(result, out, done)
-    final.start()
     for q in range(NCHUNK):
         gone = arrived.at[q, pl.ds(0, 60)]
         pltpu.make_async_copy(gone, gone, s1.at[q]).wait()
@@ -502,17 +493,34 @@
         pltpu.make_async_copy(gone, gone, s2.at[k]).wait()
         halo(k).wait_send()
         whole(stiff_in.at[k], sk1.at[k])
+        mass_first(k, 1).wait_send()
+
+        @pl.when(xl != owner(k))
+        def _():
+            mass_first(k, 0).wait_send()
+
+    for k in range(2):
+        with jax.named_scope(f"wait_end#k={k}"):
+            whole(stiff_end.at[k], rk2.at[k])
+            whole(mass_end.at[k], rm2.at[k])
+        acc = stiff_end[k, 0].astype(jnp.float32)
+        for n in range(1, 4):
+            acc += stiff_end[k, n].astype(jnp.float32)
+        out[0, k] = acc
+        acc = mass_mid[k, z].astype(jnp.float32)
+        for n in range(3):
+            acc += mass_end[k, n].astype(jnp.float32)
+        out[1, k] = acc
+
+    for k in range(SLOTS_DEV):
         stiff_second(k, 1).wait_send()
-        mass_first(k, 1).wait_send()
 
         @pl.when(xl != owner(k))
         def _():
             stiff_second(k, 0).wait_send()
-            mass_first(k, 0).wait_send()
 
     for k in range(2):
         whole(mass_end.at[k], sm2.at[k])
-    final.wait()
 
 
 def per_device(psi_sectors, stiff_blocks, mass_blocks, harmonic_table):
@@ -523,8 +531,8 @@
     out = pl.pallas_call(
         kernel,
         out_shape=jax.ShapeDtypeStruct((2, 2, 64, 512), f32),
-        in_specs=[anywhere, anywhere, anywhere, pl.BlockSpec(memory_space=pltpu.SMEM)],
-        out_specs=pl.BlockSpec(memory_space=pl.ANY),
+        in_specs=[anywhere, anywhere, anywhere, anywhere],
+        out_specs=pl.BlockSpec(memory_space=pltpu.VMEM),
         scratch_shapes=[
             pltpu.VMEM((NCHUNK, 64, PIECE, M), bf16),
             pltpu.VMEM((NCHUNK, 64, PIECE, M), bf16),
@@ -541,7 +549,7 @@
             pltpu.VMEM((2, 4, 4, 64, WIDE), bf16),
             pltpu.VMEM((2, 4, 64, WIDE), bf16),
             pltpu.VMEM((2, 3, 64, WIDE), bf16),
-            pltpu.VMEM((2, 2, 64, WIDE), f32),
+            pltpu.SMEM((SLOTS,), jnp.int32),
             dma,
             dma((2, NBAND)),
             dma((NCHUNK,)),

time: 117 us -> 116 us (level)
  no operation moved by 1% of the time
where the time goes in v7:
time: 116 us
  Pallas kernels  114 us (98%)
  local copies, waits for them, and re-layouts  1.47 us (1%)
    pallas_call x1, Pallas kernels, per_device(): pl.pallas_call(kernel, out_shape=jax.ShapeDtypeStruct((2, 2, 64, 512), f3...  114 us

profile of v7, /device:TPU:1, one launch (start us, length us, event | category | flops | bytes accessed | tf_op | source)
XLA Modules:
  0.0 116.2 jit_solution(15477897577481160436)
XLA Ops:
  0.6 0.0 copy-start
  0.6 0.6 copy-done
  1.3 114.1 %reduce_sectors.1 = f32[2,2,64,512]{3,2,1,0:T(8,128)S(1)} custom-call(bf16[4,2048,256]{2,1,0:T(8,128)(2,1)} %psi.1, bf16[16,5,128,128]{3,2,1,0:T(8,128)(2,1)} %stiff.1, bf16[16,5,128,128]{3,2,1,0:T(8,128)(2,1)} %mass.1, s32[32]{0:T(128)S(1)} %copy-done), custom_call_target="tpu_custom_call" | custom-call | tf_op jit(solution)/shard_map/reduce_sectors/pallas_call | solution.py:531
  115.4 0.8 slice_bitcast_fusion
Async XLA Ops:
  0.6 0.7 copy-start

commit v8 on v7

--- a/solution.py
+++ b/solution.py
@@ -391,7 +391,7 @@
             def _():
                 to_owner(0).start()
 
-            for dz in (2, 1, 3):
+            for dz in (1, 3, 2):
                 z_ = (z + dz) % 4
 
                 @pl.when(z_ // 2 == rows_e)
@@ -466,7 +466,7 @@
             for n in range(1, 4):
                 acc += mass_in[k % 2, n].astype(jnp.float32)
             mass_mid[k % 2] = acc.astype(jnp.bfloat16)
-            for dz in (2, 1, 3):
+            for dz in (1, 3, 2):
                 mass_second(k, dz).start()
 
         @pl.when(xl != owner(k))

time: 116 us -> 116 us (level)
  no operation moved by 1% of the time
where the time goes in v8:
time: 116 us
  Pallas kernels  114 us (98%)
  local copies, waits for them, and re-layouts  1.47 us (1%)
    pallas_call x1, Pallas kernels, per_device(): pl.pallas_call(kernel, out_shape=jax.ShapeDtypeStruct((2, 2, 64, 512), f3...  114 us

profile of v8, /device:TPU:1, one launch (start us, length us, event | category | flops | bytes accessed | tf_op | source)
XLA Modules:
  0.0 115.7 jit_solution(10397551084545371764)
XLA Ops:
  0.6 0.0 copy-start
  0.6 0.6 copy-done
  1.3 113.6 %reduce_sectors.1 = f32[2,2,64,512]{3,2,1,0:T(8,128)S(1)} custom-call(bf16[4,2048,256]{2,1,0:T(8,128)(2,1)} %psi.1, bf16[16,5,128,128]{3,2,1,0:T(8,128)(2,1)} %stiff.1, bf16[16,5,128,128]{3,2,1,0:T(8,128)(2,1)} %mass.1, s32[32]{0:T(128)S(1)} %copy-done), custom_call_target="tpu_custom_call" | custom-call | tf_op jit(solution)/shard_map/reduce_sectors/pallas_call | solution.py:531
  114.9 0.8 slice_bitcast_fusion
Async XLA Ops:
  0.6 0.7 copy-start

commit v9 on v8

--- a/solution.py
+++ b/solution.py
@@ -377,7 +377,6 @@
                     device_id_type=MESH,
                 )
 
-            to_owner(1).start()
 
             @pl.when(xl == owner(k))
             def _():
@@ -390,6 +389,8 @@
             @pl.when(xl != owner(k))
             def _():
                 to_owner(0).start()
+
+            to_owner(1).start()
 
             for dz in (1, 3, 2):
                 z_ = (z + dz) % 4

time: 116 us -> 116 us (level)
  no operation moved by 1% of the time
where the time goes in v9:
time: 116 us
  Pallas kernels  114 us (98%)
  local copies, waits for them, and re-layouts  1.47 us (1%)
    pallas_call x1, Pallas kernels, per_device(): pl.pallas_call(kernel, out_shape=jax.ShapeDtypeStruct((2, 2, 64, 512), f3...  114 us

profile of v9, /device:TPU:1, one launch (start us, length us, event | category | flops | bytes accessed | tf_op | source)
XLA Modules:
  0.0 115.8 jit_solution(11438083921188286667)
XLA Ops:
  0.6 0.0 copy-start
  0.6 0.6 copy-done
  1.3 113.7 %reduce_sectors.1 = f32[2,2,64,512]{3,2,1,0:T(8,128)S(1)} custom-call(bf16[4,2048,256]{2,1,0:T(8,128)(2,1)} %psi.1, bf16[16,5,128,128]{3,2,1,0:T(8,128)(2,1)} %stiff.1, bf16[16,5,128,128]{3,2,1,0:T(8,128)(2,1)} %mass.1, s32[32]{0:T(128)S(1)} %copy-done), custom_call_target="tpu_custom_call" | custom-call | tf_op jit(solution)/shard_map/reduce_sectors/pallas_call | solution.py:532
  114.9 0.8 slice_bitcast_fusion
Async XLA Ops:
  0.6 0.7 copy-start
